TPU v7x, 256 devices: a whole 4x4x8 slice. The times are simulated.
256 devices in a mesh: rep: 1, dp: 256 (over x, y, z, core).
Axes of the slice: x: 4, y: 4, z: 8, core: 2. Of those that a mesh axis runs over, the one named last changes fastest.
Arguments:
- x: bfloat16 [256, 1024, 768], P(('rep', 'dp'))
- dy: bfloat16 [256, 1024, 768], P(('rep', 'dp'))
- w_gate: bfloat16 [2, 768, 3072], replicated
- w_up: bfloat16 [2, 768, 3072], replicated
- w_down: bfloat16 [2, 3072, 768], replicated
- m_w_gate: float32 [2, 768, 3072], replicated
- m_w_up: float32 [2, 768, 3072], replicated
- m_w_down: float32 [2, 3072, 768], replicated
- v_w_gate: float32 [2, 768, 3072], replicated
- v_w_up: float32 [2, 768, 3072], replicated
- v_w_down: float32 [2, 3072, 768], replicated
Outputs:
- output 1: bfloat16 [2, 768, 3072], P('rep')
- output 2: bfloat16 [2, 768, 3072], P('rep')
- output 3: bfloat16 [2, 3072, 768], P('rep')
- output 4: float32 [2, 768, 3072], P('rep')
- output 5: float32 [2, 768, 3072], P('rep')
- output 6: float32 [2, 3072, 768], P('rep')
- output 7: float32 [2, 768, 3072], P('rep')
- output 8: float32 [2, 768, 3072], P('rep')
- output 9: float32 [2, 3072, 768], P('rep')
All inputs are finite; a program needn't handle non-finite values.
Results may differ from a plain program's by a relative error of at most 0.022.
Values are sent between devices in bfloat16 or wider.
A program may use at most 768 MiB of HBM per device.

v0:
```python
import jax
import jax.numpy as jnp
from jax import lax
from jax.sharding import PartitionSpec as P

NAMES = ("w_gate", "w_up", "w_down")


def matmul(a, w):
    return jnp.dot(a, w, preferred_element_type=jnp.float32).astype(jnp.bfloat16)


def normed(h):
    wide = h.astype(jnp.float32)
    scale = lax.rsqrt(jnp.mean(wide**2, -1, keepdims=True) + 1e-6)
    return (wide * scale).astype(jnp.bfloat16)


def layer(h, w):
    a = normed(h)
    gate = jnp.dot(a, w["w_gate"], preferred_element_type=jnp.float32)
    up = jnp.dot(a, w["w_up"], preferred_element_type=jnp.float32)
    return h + matmul((jax.nn.silu(gate) * up).astype(jnp.bfloat16), w["w_down"])


def adamw(w, m, v, g):
    m = 0.9 * m + 0.1 * g
    v = 0.95 * v + 0.05 * g * g
    step = m * lax.rsqrt(v + 1e-8) + 0.1 * w
    return (w - 0.02 * step).astype(jnp.bfloat16), m, v


def solution(mesh):
    def step(x, dy, *arrays):
        weights, m, v = (arrays[i : i + 3] for i in (0, 3, 6))
        layers = weights[0].shape[0]
        h, kept = x[0], []
        for number in range(layers):
            kept.append(h)
            h = layer(h, {name: w[number] for name, w in zip(NAMES, weights, strict=True)})
        by_h, summed = dy[0], [None] * layers
        for number in reversed(range(layers)):
            _, back = jax.vjp(lambda w, h: layer(h, w), {name: w[number] for name, w in zip(NAMES, weights, strict=True)}, kept[number])
            by_w, by_h = back(by_h)
            summed[number] = [lax.psum(by_w[name], "dp") for name in NAMES]
        gradients = [jnp.stack([summed[number][i] for number in range(layers)]).astype(jnp.float32) for i in range(3)]
        new = [adamw(w.astype(jnp.float32), m, v, g) for w, m, v, g in zip(weights, m, v, gradients, strict=True)]
        return tuple(one[which] for which in range(3) for one in new)

    return jax.shard_map(
        step,
        mesh=mesh,
        in_specs=(P(("rep", "dp"), None, None),) * 2 + (P(None, None, None),) * 9,
        out_specs=(P("rep", None, None),) * 9,
        check_vma=False,
    )
```

profile of v0, /device:TPU:1, one launch (start us, length us, event | category | flops | bytes accessed | tf_op | source)
XLA Modules:
  0.0 689.6 jit_solution(5812391269902690979)
XLA Ops:
  7.2 0.0 all-reduce.3.cloned.1.call-start
  7.2 1.7 copy.20
  8.9 0.0 copy-start
  9.0 0.4 fusion.68
  9.3 2.8 copy.21
  12.1 9.2 %convolution_convert_fusion.1 = bf16[1024,3072]{1,0:T(8,128)(2,1)} fusion(bf16[2,3072,768]{2,1,0:T(8,128)(2,1)} %param.15, bf16[1,1024,768]{2,1,0:T(8,128)(2,1)} %param.12), kind=kOutput, calls=%fused_computation.55 | convolution fusion | flops 4834983936 | bytes 12582912 | tf_op jit(solution)/shard_map/transpose(jvp())/dot_general | solution.py:10
  21.3 0.0 copy-done.4
  21.3 10.6 %fusion.49 = f32[1024,3072]{1,0:T(8,128)} fusion(bf16[2,768,3072]{2,1,0:T(8,128)(2,1)} %param.13, bf16[1,1024,768]{2,1,0:T(8,128)(2,1)S(1)} %copy-done.4, f32[1024]{0:T(1024)S(1)} %add_rsqrt_fusion), kind=kOutput, calls=%fused_computation.79 | convolution fusion | flops 4834197504 | bytes 18878464 | tf_op jit(solution)/shard_map/dot_general | solution.py:21
  31.9 0.0 copy-done.8
  31.9 0.0 slice-done
  31.9 0.0 slice-done.1
  32.0 0.0 slice-done.2
  32.0 12.4 %multiply_convert_fusion.1 = (bf16[1024,3072]{1,0:T(8,128)(2,1)}, f32[1024,3072]{1,0:T(8,128)}) fusion(f32[1024,3072]{1,0:T(8,128)} %fusion.49, bf16[2,768,3072]{2,1,0:T(8,128)(2,1)S(1)} %bitcast.81, bf16[1,1024,768]{2,1,0:T(8,128)(2,1)S(1)} %copy-done.4, f32[1024]{0:T(1024)S(1)} %add_rsqrt_fusion), kind=kOutput, calls=%fused_computation.44 | convolution fusion | flops 4853071872 | bytes 37752832 | tf_op jit(solution)/shard_map/dot_general | solution.py:22
  44.4 0.0 copy-done
  44.4 8.8 %fusion.72 = (f32[1024]{0:T(1024)S(1)}, bf16[1024,768]{0,1:T(8,128)(2,1)S(1)}) fusion(bf16[1024,3072]{1,0:T(8,128)(2,1)} %get-tuple-element.24, bf16[2,3072,768]{2,1,0:T(8,128)(2,1)} %param.15, bf16[1,1024,768]{1,2,0:T(8,128)(2,1)S(1)} %copy.20), kind=kOutput, calls=%fused_computation.103 | convolution fusion | flops 4835769344 | bytes 14159872 | tf_op jit(solution)/shard_map/dot_general | solution.py:10
  53.1 0.0 copy-start.6
  53.2 8.3 %fusion.36 = f32[1024,3072]{1,0:T(8,128)} fusion(bf16[2,768,3072]{2,1,0:T(8,128)(2,1)S(1)} %bitcast.81, bf16[1024,768]{0,1:T(8,128)(2,1)S(1)} %get-tuple-element.27, f32[1024]{0:T(1024)S(1)} %fusion.102), kind=kOutput, calls=%fused_computation.66 | convolution fusion | flops 4834197504 | bytes 18878464 | tf_op jit(solution)/shard_map/jvp()/dot_general | solution.py:22
  61.5 0.0 copy-done.6
  61.5 18.2 %fusion.17 = (bf16[1024,3072]{1,0:T(8,128)(2,1)}, f32[1024,3072]{1,0:T(8,128)}) fusion(f32[1024,3072]{1,0:T(8,128)} %fusion.36, bf16[1024,3072]{1,0:T(8,128)(2,1)} %convolution_convert_fusion.1, bf16[2,768,3072]{2,1,0:T(8,128)(2,1)} %param.13, bf16[1024,768]{0,1:T(8,128)(2,1)S(1)} %get-tuple-element.27, f32[1024]{0:T(1024)S(1)} %fusion.102), kind=kOutput, calls=%fused_computation.35 | convolution fusion | flops 4871946240 | bytes 44044288 | tf_op jit(solution)/shard_map/jvp()/dot_general | solution.py:21
  79.7 11.6 %fusion.82 = bf16[1024,768]{0,1:T(8,128)(2,1)} fusion(bf16[2,768,3072]{2,1,0:T(8,128)(2,1)} %param.14, bf16[1024,3072]{1,0:T(8,128)(2,1)} %convolution_convert_fusion.1, f32[1024,3072]{1,0:T(8,128)} %get-tuple-element.29), kind=kOutput, calls=%fused_computation.109 | convolution fusion | flops 4851499008 | bytes 25165824 | tf_op jit(solution)/shard_map/transpose(jvp())/dot_general | solution.py:22
  91.3 11.3 %fusion.55 = bf16[1,768,3072]{2,1,0:T(8,128)(2,1)} fusion(bf16[1024,3072]{1,0:T(8,128)(2,1)} %convolution_convert_fusion.1, bf16[1024,768]{0,1:T(8,128)(2,1)S(1)} %get-tuple-element.27, f32[1024]{0:T(1024)S(1)} %fusion.102, f32[1024,3072]{1,0:T(8,128)} %get-tuple-element.29), kind=kOutput, calls=%fused_computation.85 | convolution fusion | flops 4855431168 | bytes 25169920 | tf_op jit(solution)/shard_map/transpose(jvp())/dot_general | solution.py:22
  102.5 0.0 slice-done.3
  102.5 0.0 slice-done.4
  102.5 0.0 slice-done.5
  102.5 0.0 copy-done.5
  102.6 11.5 %fusion.56 = bf16[1,3072,768]{2,1,0:T(8,128)(2,1)} fusion(f32[1024,3072]{1,0:T(8,128)S(1)} %bitcast.83, bf16[1,1024,768]{2,1,0:T(8,128)(2,1)S(1)} %copy-done.5, f32[1024,3072]{1,0:T(8,128)} %get-tuple-element.29), kind=kOutput, calls=%fused_computation.86 | convolution fusion | flops 4853071872 | bytes 31457280 | tf_op jit(solution)/shard_map/transpose(jvp())/dot_general | solution.py:10
  114.1 9.6 %fusion.57 = bf16[1,768,3072]{2,1,0:T(8,128)(2,1)} fusion(bf16[1024,3072]{1,0:T(8,128)(2,1)} %get-tuple-element.28, bf16[1024,768]{0,1:T(8,128)(2,1)S(1)} %get-tuple-element.27, f32[1024]{0:T(1024)S(1)} %fusion.102), kind=kOutput, calls=%fused_computation.87 | convolution fusion | flops 4834197504 | bytes 12587008 | tf_op jit(solution)/shard_map/transpose(jvp())/dot_general | solution.py:21
  123.7 0.0 copy-done.10
  123.7 0.0 copy-done.11
  123.7 0.0 copy-start.2
  123.7 0.0 slice-start.8
  123.7 7.4 %fusion.74 = (f32[1024]{0:T(1024)S(1)}, bf16[1024,768]{0,1:T(8,128)(2,1)S(1)}) fusion(bf16[1024,768]{0,1:T(8,128)(2,1)S(1)} %get-tuple-element.27, bf16[1024,768]{0,1:T(8,128)(2,1)S(1)} %copy-done.11, bf16[1024,3072]{1,0:T(8,128)(2,1)S(1)} %copy-done.10, bf16[2,768,3072]{2,1,0:T(8,128)(2,1)} %param.13), kind=kOutput, calls=%fused_computation.105 | convolution fusion | flops 4835769344 | bytes 15732736 | tf_op jit(solution)/shard_map/transpose(jvp())/dot_general | solution.py:21
  131.1 0.0 copy-done.7
  131.1 0.0 copy-done.2
  131.1 1.1 fusion.86
  132.3 0.0 slice-done.6
  132.3 0.0 slice-start.9
  132.3 0.0 slice-start.10
  132.3 5.6 convolution_convert_fusion
  137.9 0.0 slice-start.11
  137.9 9.9 %fusion.58 = bf16[1,3072,768]{2,1,0:T(8,128)(2,1)} fusion(bf16[1024,3072]{1,0:T(8,128)(2,1)} %get-tuple-element.24, bf16[1024,768]{0,1:T(8,128)(2,1)S(1)} %fusion.86), kind=kOutput, calls=%fused_computation.88 | convolution fusion | flops 4834197504 | bytes 12582912 | tf_op jit(solution)/shard_map/transpose(jvp())/dot_general | solution.py:10
  147.8 0.0 slice-done.10
  147.9 7.1 %fusion.54 = bf16[1,768,3072]{2,1,0:T(8,128)(2,1)} fusion(bf16[1024,3072]{1,0:T(8,128)(2,1)S(1)} %convolution_convert_fusion, f32[1024,3072]{1,0:T(8,128)S(1)} %bitcast.87, bf16[1,1024,768]{1,2,0:T(8,128)(2,1)S(1)} %copy-done.1, f32[1024]{0:T(1024)S(1)} %copy-done.9), kind=kOutput, calls=%fused_computation.84 | convolution fusion | flops 4855431168 | bytes 25169920 | tf_op jit(solution)/shard_map/transpose(jvp())/dot_general | solution.py:22
  155.0 13.0 %fusion.59 = bf16[1,768,3072]{2,1,0:T(8,128)(2,1)} fusion(f32[1024,3072]{1,0:T(8,128)} %fusion.49, f32[1024,3072]{1,0:T(8,128)} %get-tuple-element.25, bf16[1024,3072]{1,0:T(8,128)(2,1)S(1)} %convolution_convert_fusion, bf16[1,1024,768]{1,2,0:T(8,128)(2,1)S(1)} %copy-done.1, f32[1024]{0:T(1024)S(1)} %copy-done.9), kind=kOutput, calls=%fused_computation.89 | convolution fusion | flops 4871159808 | bytes 37752832 | tf_op jit(solution)/shard_map/transpose(jvp())/dot_general | solution.py:21
  168.0 0.0 all-reduce.3.cloned.1.call-update
  168.0 414.8 %all-reduce.3.cloned.1.call-done = (bf16[1,768,3072]{2,1,0:T(8,128)(2,1)}, bf16[1,768,3072]{2,1,0:T(8,128)(2,1)}, bf16[1,768,3072]{2,1,0:T(8,128)(2,1)}, bf16[1,...) async-done(((bf16[1,768,3072]{2,1,0:T(8,128)(2,1)}, bf16[1,768,3072]{2,1,0:T(8,128)(2,1)}, bf16[1,768,3072]{2,1,0:T(8,128)(2,1)}, ...) | async-done | bytes 28311568 | tf_op jit(solution)/shard_map/psum | solution.py:45
  582.9 36.6 %fusion.10 = (bf16[2,3072,768]{2,1,0:T(8,128)(2,1)}, f32[2,3072,768]{2,1,0:T(8,128)}, f32[2,3072,768]{2,1,0:T(8,128)}) fusion(bf16[2,3072,768]{2,1,0:T(8,128)(2,1)} %param.15, bf16[1,3072,768]{2,1,0:T(8,128)(2,1)} %get-tuple-element.13, bf16[1,3072,768]{2,1,0:T(8,128)(2,1)} %get-tuple-element.14, f32[2,3072,768]{2,1,0:T(8,128)} %param.21, ...), kind=kLoop, calls=%fused_computation.24 | loop fusion | flops 89653248 | bytes 103809024 | tf_op jit(solution)/shard_map/convert_element_type | solution.py:30
  619.5 63.1 %fusion.2 = (bf16[2,768,3072]{2,1,0:T(8,128)(2,1)}, f32[2,768,3072]{2,1,0:T(8,128)}, f32[2,768,3072]{2,1,0:T(8,128)}, bf16[2,768,3072]{2,1,0:T(8,128)(2,1)}, f32...) fusion(bf16[2,768,3072]{2,1,0:T(8,128)(2,1)} %param.13, bf16[1,768,3072]{2,1,0:T(8,128)(2,1)S(1)} %copy-done.3, ...), kind=kLoop, calls=%fused_computation.16 | loop fusion | flops 179306496 | bytes 207618048 | tf_op jit(solution)/shard_map/convert_element_type | solution.py:30
  (31 shorter events, 0.1 us)
Async XLA Ops:
  7.2 575.7 %all-reduce.3.cloned.1.call-start = ((), (), s32[]{:S(2)}) async-start(), calls=%async_computation | async-start | bytes 56623104 | tf_op jit(solution)/shard_map/psum | solution.py:45
  8.9 35.4 %copy-start = (bf16[1,1024,768]{1,2,0:T(8,128)(2,1)}, bf16[1,1024,768]{1,2,0:T(8,128)(2,1)S(1)}, u32[]{:S(2)}) copy-start(bf16[1,1024,768]{1,2,0:T(8,128)(2,1)S(1)} %copy.20) | copy-start | bytes 4718596
  9.3 22.6 %copy-start.8 = (f32[1024]{0:T(1024)}, f32[1024]{0:T(1024)S(1)}, u32[]{:S(2)}) copy-start(f32[1024]{0:T(1024)S(1)} %add_rsqrt_fusion) | copy-start | bytes 12292
  12.1 9.2 %copy-start.4 = (bf16[1,1024,768]{2,1,0:T(8,128)(2,1)S(1)}, bf16[1,1024,768]{2,1,0:T(8,128)(2,1)}, u32[]{:S(2)}) copy-start(bf16[1,1024,768]{2,1,0:T(8,128)(2,1)} %param.11) | copy-start | bytes 4718596
  12.1 19.9 %slice-start = ((s8[9437184]{0:T(1024)(128)(4,1)}), s8[4194304]{0:T(1024)(128)(4,1)S(1)}, s32[]{:S(2)}) async-start(s8[9437184]{0:T(1024)(128)(4,1)} %bitcast.80), calls=%async_computation.1 | async-start | bytes 8388608
  12.1 19.9 %slice-start.1 = ((s8[9437184]{0:T(1024)(128)(4,1)}), s8[4194304]{0:T(1024)(128)(4,1)S(1)}, s32[]{:S(2)}) async-start(s8[9437184]{0:T(1024)(128)(4,1)} %bitcast.80), calls=%async_computation.2 | async-start | bytes 8388608
  21.3 10.6 %slice-start.2 = ((s8[9437184]{0:T(1024)(128)(4,1)}), s8[1048576]{0:T(1024)(128)(4,1)S(1)}, s32[]{:S(2)}) async-start(s8[9437184]{0:T(1024)(128)(4,1)} %bitcast.80), calls=%async_computation.3 | async-start | bytes 2097152
  53.1 8.3 %copy-start.6 = (f32[1024]{0:T(1024)}, f32[1024]{0:T(1024)S(1)}, u32[]{:S(2)}) copy-start(f32[1024]{0:T(1024)S(1)} %get-tuple-element.26) | copy-start | bytes 12292
  79.7 22.8 %slice-start.3 = ((s8[12582912]{0:T(1024)(128)(4,1)}), s8[4194304]{0:T(1024)(128)(4,1)S(1)}, s32[]{:S(2)}) async-start(s8[12582912]{0:T(1024)(128)(4,1)} %bitcast.82), calls=%async_computation.4 | async-start | bytes 8388608
  79.7 22.8 %slice-start.4 = ((s8[12582912]{0:T(1024)(128)(4,1)}), s8[4194304]{0:T(1024)(128)(4,1)S(1)}, s32[]{:S(2)}) async-start(s8[12582912]{0:T(1024)(128)(4,1)} %bitcast.82), calls=%async_computation.5 | async-start | bytes 8388608
  91.3 11.3 %slice-start.5 = ((s8[12582912]{0:T(1024)(128)(4,1)}), s8[4194304]{0:T(1024)(128)(4,1)S(1)}, s32[]{:S(2)}) async-start(s8[12582912]{0:T(1024)(128)(4,1)} %bitcast.82), calls=%async_computation.6 | async-start | bytes 8388608
  91.3 11.3 %copy-start.5 = (bf16[1,1024,768]{2,1,0:T(8,128)(2,1)S(1)}, bf16[1,1024,768]{2,1,0:T(8,128)(2,1)}, u32[]{:S(2)}) copy-start(bf16[1,1024,768]{2,1,0:T(8,128)(2,1)} %param.12) | copy-start | bytes 4718596
  114.1 9.6 %copy-start.10 = (bf16[1024,3072]{1,0:T(8,128)(2,1)S(1)}, bf16[1024,3072]{1,0:T(8,128)(2,1)}, u32[]{:S(2)}) copy-start(bf16[1024,3072]{1,0:T(8,128)(2,1)} %get-tuple-element.28) | copy-start | bytes 18874372
  114.1 9.6 %copy-start.11 = (bf16[1024,768]{0,1:T(8,128)(2,1)S(1)}, bf16[1024,768]{0,1:T(8,128)(2,1)}, u32[]{:S(2)}) copy-start(bf16[1024,768]{0,1:T(8,128)(2,1)} %fusion.82) | copy-start | bytes 4718596
  114.1 18.2 %slice-start.6 = ((s8[9437184]{0:T(1024)(128)(4,1)}), s8[4194304]{0:T(1024)(128)(4,1)S(1)}, s32[]{:S(2)}) async-start(s8[9437184]{0:T(1024)(128)(4,1)} %bitcast.84), calls=%async_computation.7 | async-start | bytes 8388608
  114.1 18.2 %slice-start.7 = ((s8[9437184]{0:T(1024)(128)(4,1)}), s8[4194304]{0:T(1024)(128)(4,1)S(1)}, s32[]{:S(2)}) async-start(s8[9437184]{0:T(1024)(128)(4,1)} %bitcast.84), calls=%async_computation.8 | async-start | bytes 8388608
  123.7 7.4 %copy-start.7 = (f32[1024]{0:T(1024)S(1)}, f32[1024]{0:T(1024)}, u32[]{:S(2)}) copy-start(f32[1024]{0:T(1024)} %copy-done.6) | copy-start | bytes 12292
  123.7 7.4 %copy-start.2 = (bf16[1,1024,768]{1,2,0:T(8,128)(2,1)S(1)}, bf16[1,1024,768]{1,2,0:T(8,128)(2,1)}, u32[]{:S(2)}) copy-start(bf16[1,1024,768]{1,2,0:T(8,128)(2,1)} %copy.21) | copy-start | bytes 4718596
  123.7 8.6 %slice-start.8 = ((s8[9437184]{0:T(1024)(128)(4,1)}), s8[1048576]{0:T(1024)(128)(4,1)S(1)}, s32[]{:S(2)}) async-start(s8[9437184]{0:T(1024)(128)(4,1)} %bitcast.84), calls=%async_computation.9 | async-start | bytes 2097152
  132.3 15.5 %slice-start.9 = ((s8[12582912]{0:T(1024)(128)(4,1)}), s8[4194304]{0:T(1024)(128)(4,1)S(1)}, s32[]{:S(2)}) async-start(s8[12582912]{0:T(1024)(128)(4,1)} %bitcast.86), calls=%async_computation.10 | async-start | bytes 8388608
  132.3 15.5 %slice-start.10 = ((s8[12582912]{0:T(1024)(128)(4,1)}), s8[4194304]{0:T(1024)(128)(4,1)S(1)}, s32[]{:S(2)}) async-start(s8[12582912]{0:T(1024)(128)(4,1)} %bitcast.86), calls=%async_computation.11 | async-start | bytes 8388608
  137.9 10.0 %copy-start.1 = (bf16[1,1024,768]{1,2,0:T(8,128)(2,1)S(1)}, bf16[1,1024,768]{1,2,0:T(8,128)(2,1)}, u32[]{:S(2)}) copy-start(bf16[1,1024,768]{1,2,0:T(8,128)(2,1)} %copy-done) | copy-start | bytes 4718596
  137.9 10.0 %copy-start.9 = (f32[1024]{0:T(1024)S(1)}, f32[1024]{0:T(1024)}, u32[]{:S(2)}) copy-start(f32[1024]{0:T(1024)} %copy-done.8) | copy-start | bytes 12292
  137.9 10.0 %slice-start.11 = ((s8[12582912]{0:T(1024)(128)(4,1)}), s8[4194304]{0:T(1024)(128)(4,1)S(1)}, s32[]{:S(2)}) async-start(s8[12582912]{0:T(1024)(128)(4,1)} %bitcast.86), calls=%async_computation.12 | async-start | bytes 8388608
  582.9 36.6 %copy-start.3 = (bf16[1,768,3072]{2,1,0:T(8,128)(2,1)S(1)}, bf16[1,768,3072]{2,1,0:T(8,128)(2,1)}, u32[]{:S(2)}) copy-start(bf16[1,768,3072]{2,1,0:T(8,128)(2,1)} %get-tuple-element.9) | copy-start | bytes 14155780
Sparse Core Ops, SparseCore 0:
  168.2 414.6 all-reduce.2
where the time goes:
time: 698 us; the launch traced here: 690 us
  waiting for transfers between devices  415 us (59%)
  matrix products  154 us (22%)
  other arithmetic  101 us (14%)
  between operations  14.5 us (2%)
    psum x1, waiting for transfers between devices, step(): summed[number] = [lax.psum(by_w[name], 'dp') for name in NAMES]  415 us
    convert_element_type x2, other arithmetic, adamw(): return ((w - 0.02 * step).astype(jnp.bfloat16), m, v)  99.7 us
    dot_general x5, matrix products, layer(): gate = jnp.dot(a, w['w_gate'], preferred_element_type=jnp.float32)  58.8 us
    dot_general x5, matrix products, layer(): up = jnp.dot(a, w['w_up'], preferred_element_type=jnp.float32)  50.7 us
    dot_general x5, matrix products, matmul(): jnp.dot(a, w, preferred_element_type=jnp.float32).astype(jnp.bfloat16)  45 us
  transfers between devices with their start and end apart: 1, of which 1 were waited for; matrix products, arithmetic and copies ran while one was open for 0% of the time, Pallas kernels for 0%

commit v1 on v0

--- a/solution.py
+++ b/solution.py
@@ -1,11 +1,354 @@
+import functools
+
 import jax
 import jax.numpy as jnp
 from jax import lax
+from jax.experimental import pallas as pl
+from jax.experimental.pallas import tpu as pltpu
 from jax.sharding import PartitionSpec as P
 
 NAMES = ("w_gate", "w_up", "w_down")
-
-
+MESH = pl.DeviceIdType.MESH
+F32, BF16 = jnp.float32, jnp.bfloat16
+LANES = 128
+
+def chunk_of(n, cap=128):
+    best = 16
+    for c in range(16, cap + 1, 16):
+        if n % c == 0:
+            best = c
+    return best
+
+def over_rows(n, body, cap=128):
+    c = chunk_of(n, cap)
+    if n == c:
+        body(0, c)
+    else:
+        def step(i, _):
+            body(pl.multiple_of(i * c, 16), c)
+            return 0
+        lax.fori_loop(0, n // c, step, 0)
+
+class Color:
+    def __init__(self, name, off, S, dims, n):
+        self.name, self.off, self.S, self.dims = name, off, S, dims
+        self.n1, self.n2, self.n3 = (n[d] for d in dims)
+        self.L = S // self.n1
+        self.La = (self.L // 2) // 16 * 16
+        self.Lb = self.L - self.La
+        self.L2 = self.L // self.n2
+        self.La2 = (self.L2 // 2) // 16 * 16
+        self.Lb2 = self.L2 - self.La2
+        assert S % (self.n1 * self.n2 * 16) == 0 and self.Lb % self.L2 == 0 and self.La2 > 0, (S, self.L, self.L2)
+        h1, h2 = self.n1 // 2, self.n2 // 2
+        self.h1, self.h2 = h1, h2
+        self.m_rs1, self.m_rs2 = 0, 2 * h1
+        self.m_y = self.m_rs2 + 2 * h2
+        self.m_ag2 = self.m_y + self.n3 - 1
+        self.m_ag1 = self.m_ag2 + 2 * h2
+        self.m_pair = self.m_ag1 + 2 * h1
+        self.nmsg = self.m_pair + 1
+    def scratch(self, NB):
+        return [pltpu.VMEM((NB, (self.n1 - 1) * self.L, LANES), BF16),
+                pltpu.VMEM((NB, self.L, LANES), F32),
+                pltpu.VMEM((NB, self.L, LANES), BF16),
+                pltpu.VMEM((NB, (self.n2 - 1) * self.L2, LANES), BF16),
+                pltpu.VMEM((NB, self.L2, LANES), F32),
+                pltpu.VMEM((NB, self.n3, self.L2, LANES), BF16),
+                pltpu.SemaphoreType.DMA((NB, self.nmsg)), pltpu.SemaphoreType.DMA((NB, self.nmsg))]
+
+def m16(v):
+    return pl.multiple_of(v, 16)
+
+class Comm:
+    def __init__(self, n, cfg, B, NB):
+        self.n, self.B, self.NB = n, B, NB
+        off, self.colors = 0, []
+        for name, rows, dims in cfg:
+            self.colors.append(Color(name, off, rows, dims, n)); off += rows
+        self.HB, self.TB = off, 2 * off
+    def scratch(self):
+        out = [pltpu.VMEM((self.B, self.TB, LANES), BF16), pltpu.VMEM((self.NB, self.HB, LANES), BF16),
+               pltpu.SemaphoreType.DMA((self.NB,)), pltpu.SemaphoreType.DMA((self.NB,))]
+        for c in self.colors:
+            out += c.scratch(self.NB)
+        return out
+    def setup(self, scratch):
+        n = self.n
+        me = lax.axis_index("dp")
+        core = lax.rem(me, 2); z = lax.rem(lax.div(me, 2), n["z"])
+        y = lax.rem(lax.div(me, 2 * n["z"]), n["y"]); x = lax.div(me, 2 * n["z"] * n["y"])
+        self.pos = {"x": x, "y": y, "z": z}
+        self.core = core
+        stride = {"x": 2 * n["z"] * n["y"], "y": 2 * n["z"], "z": 2}
+        def shifted(d, k):
+            q = lax.rem(self.pos[d] + k + n[d], n[d])
+            return me + (q - self.pos[d]) * stride[d]
+        self.shifted = shifted
+        self.partner = me + 1 - 2 * core
+        self.G, self.D, self.ds, self.dr = scratch[:4]
+        self.bufs = {}
+        rest = scratch[4:]
+        for i, c in enumerate(self.colors):
+            self.bufs[c.name] = rest[8 * i:8 * i + 8]
+        self.mine = core * self.HB
+        self.other = (1 - core) * self.HB
+    def barrier(self):
+        n = self.n
+        peers = [self.partner]
+        need = {d: set() for d in "xyz"}
+        for c in self.colors:
+            for d in c.dims[:2]:
+                need[d] |= {1 % n[d], (n[d] - 1) % n[d]}
+            need[c.dims[2]] |= set(range(1, n[c.dims[2]]))
+        for d in "xyz":
+            for k in sorted(need[d]):
+                if k:
+                    peers.append(self.shifted(d, k))
+        sem = pltpu.get_barrier_semaphore()
+        for p in peers:
+            pl.semaphore_signal(sem, inc=1, device_id={"dp": p}, device_id_type=MESH)
+        pl.semaphore_wait(sem, len(peers))
+    def copy(self, src, dst, ss, rs, dev):
+        return pltpu.make_async_remote_copy(src_ref=src, dst_ref=dst, send_sem=ss, recv_sem=rs, device_id={"dp": dev}, device_id_type=MESH)
+
+    def pair_copy(self, b):
+        s = lax.rem(b, self.NB)
+        return self.copy(self.G.at[b, pl.ds(m16(self.other), self.HB)], self.D.at[s], self.ds.at[s], self.dr.at[s], self.partner)
+    def phases(self):
+        out = [[lambda b: self.pair_copy(b).start()], [lambda b: self.pair_copy(b).wait()]]
+        per = [self.color_phases(c) for c in self.colors]
+        depth = max(len(p) for p in per)
+        out += [[] for _ in range(depth - 1)]
+        for p in per:
+            for i, f in enumerate(p):
+                out[1 + i].append(f)
+        return out
+
+    def color_phases(self, c):
+        G, D = self.G, self.D
+        R1, O1, O1b, R2, O2, Y, SS, RS = self.bufs[c.name]
+        NB = self.NB
+        p1, p2, p3 = (self.pos[d] for d in c.dims)
+        r1, l1 = self.shifted(c.dims[0], 1), self.shifted(c.dims[0], -1)
+        r2, l2 = self.shifted(c.dims[1], 1), self.shifted(c.dims[1], -1)
+        n1, n2, n3, h1, h2 = c.n1, c.n2, c.n3, c.h1, c.h2
+        L, La, Lb, L2, La2, Lb2 = c.L, c.La, c.Lb, c.L2, c.La2, c.Lb2
+        mod = lambda v, n: lax.rem(v + 4 * n, n)
+        base = self.mine + c.off
+        dbase = c.off
+        sl = lambda b: lax.rem(b, NB)
+
+        def ring(stage):
+            if stage == 1:
+                return dict(n=n1, h=h1, L=L, La=La, Lb=Lb, p=p1, right=r1, left=l1, R=R1, m=c.m_rs1)
+            return dict(n=n2, h=h2, L=L2, La=La2, Lb=Lb2, p=p2, right=r2, left=l2, R=R2, m=c.m_rs2)
+        def local(stage, b, row, k):
+            if stage == 1:
+                return G[b, pl.ds(m16(base + row), k), :].astype(F32) + D[sl(b), pl.ds(m16(dbase + row), k), :].astype(F32)
+            return O1[sl(b), pl.ds(m16(row), k), :] + R1[sl(b), pl.ds(m16(2 * (h1 - 1) * L + row), k), :].astype(F32)
+        def staged(stage, b, row, k):
+            if stage == 1:
+                return D.at[sl(b), pl.ds(m16(dbase + row), k)]
+            return O1b.at[sl(b), pl.ds(m16(row), k)]
+        def rs_copy(stage, b, k, direction):
+            g = ring(stage)
+            n, h, LL, A, Bb = g["n"], g["h"], g["L"], g["La"], g["Lb"]
+            s = sl(b)
+            if k < h:
+                slot = mod(g["p"] + h - k + 1, n) if direction == 0 else mod(g["p"] - h + k, n)
+                src = staged(stage, b, slot * LL, LL)
+                dst = g["R"].at[s, pl.ds((k - 1) * 2 * LL + direction * LL, LL)]
+            elif direction == 0:
+                src = staged(stage, b, mod(g["p"] + 1, n) * LL + A, Bb)
+                dst = g["R"].at[s, pl.ds((h - 1) * 2 * LL, Bb)]
+            else:
+                src = staged(stage, b, g["p"] * LL, A)
+                dst = g["R"].at[s, pl.ds((h - 1) * 2 * LL + Bb, A)]
+            m = g["m"] + 2 * (k - 1) + direction
+            return self.copy(src, dst, SS.at[s, m], RS.at[s, m], g["right"] if direction == 0 else g["left"])
+        def rs_step(stage, k):
+            def f(b):
+                g = ring(stage)
+                n, h, LL, A, Bb = g["n"], g["h"], g["L"], g["La"], g["Lb"]
+                s = sl(b)
+                for direction in (0, 1):
+                    if k > 1:
+                        rs_copy(stage, b, k - 1, direction).wait()
+                    slot = mod(g["p"] + h - k + 1, n) if direction == 0 else mod(g["p"] - h + k, n)
+                    rin = (k - 2) * 2 * LL + direction * LL
+                    def total(row, at, kk):
+                        v = local(stage, b, row, kk)
+                        if k > 1:
+                            v = v + g["R"][s, pl.ds(m16(rin + at), kk), :].astype(F32)
+                        return v
+                    def send_part(lo, cnt):
+                        def body(i, kk):
+                            v = total(slot * LL + lo + i, lo + i, kk)
+                            ref = D if stage == 1 else O1b
+                            o = (dbase if stage == 1 else 0) + slot * LL + lo + i
+                            ref[s, pl.ds(m16(o), kk), :] = v.astype(BF16)
+                        over_rows(cnt, body)
+                    def keep_part(lo, cnt, to):
+                        ref = O1 if stage == 1 else O2
+                        def body(i, kk):
+                            ref[s, pl.ds(m16(to + i), kk), :] = total(slot * LL + lo + i, lo + i, kk)
+                        over_rows(cnt, body)
+                    if k < h:
+                        send_part(0, LL)
+                        rs_copy(stage, b, k, direction).start()
+                    elif direction == 0:
+                        send_part(A, Bb)
+                        rs_copy(stage, b, k, direction).start()
+                        keep_part(0, A, Bb)
+                    else:
+                        send_part(0, A)
+                        rs_copy(stage, b, k, direction).start()
+                        keep_part(A, Bb, 0)
+            return f
+        def rs_end(stage):
+            def f(b):
+                for direction in (0, 1):
+                    rs_copy(stage, b, ring(stage)["h"], direction).wait()
+            return f
+        def y_copy(b, k):
+            s = sl(b)
+            m = c.m_y + k - 1
+            return self.copy(Y.at[s, p3], Y.at[s, p3], SS.at[s, m], RS.at[s, m], self.shifted(c.dims[2], k))
+        def y_wait(b, k):
+            s = sl(b)
+            m = c.m_y + k - 1
+            return self.copy(Y.at[s, p3], Y.at[s, mod(p3 - k, n3)], SS.at[s, m], RS.at[s, m], self.shifted(c.dims[2], k))
+        def y_send(b):
+            s = sl(b)
+            def body(i, kk):
+                v = O2[s, pl.ds(i, kk), :] + R2[s, pl.ds(m16(2 * (h2 - 1) * L2 + i), kk), :].astype(F32)
+                Y[s, p3, pl.ds(i, kk), :] = v.astype(BF16)
+            over_rows(L2, body)
+            for k in range(1, n3):
+                y_copy(b, k).start()
+        def grow(v):
+            return base + mod(p1 * L + La + v, c.S)
+        def y_sum(b):
+            s = sl(b)
+            for k in range(1, n3):
+                y_wait(b, k).wait()
+            def part(src, cnt, row):
+                def body(i, kk):
+                    v = Y[s, 0, pl.ds(m16(src + i), kk), :].astype(F32)
+                    for j in range(1, n3):
+                        v = v + Y[s, j, pl.ds(m16(src + i), kk), :].astype(F32)
+                    G[b, pl.ds(m16(row + i), kk), :] = v.astype(BF16)
+                over_rows(cnt, body)
+            part(0, Lb2, grow(p2 * L2 + La2))
+            part(Lb2, La2, grow(mod(p2 + 1, n2) * L2))
+        def ag_copy(stage, b, k, direction):
+            s = sl(b)
+            if stage == 2:
+                n, LL, A, Bb, p, right, left, m = n2, L2, La2, Lb2, p2, r2, l2, c.m_ag2
+                at = lambda slot, part: grow(slot * L2) + part
+            else:
+                n, LL, A, Bb, p, right, left, m = n1, L, La, Lb, p1, r1, l1, c.m_ag1
+                at = lambda slot, part: base + slot * L + part
+            if k == 1:
+                row, cnt = (at(mod(p + 1, n), 0), A) if direction == 0 else (at(p, A), Bb)
+            else:
+                row, cnt = (at(mod(p - (k - 2), n), 0) if direction == 0 else at(mod(p + 1 + (k - 2), n), 0)), LL
+            ref = G.at[b, pl.ds(m16(row), cnt)]
+            mm = m + 2 * (k - 1) + direction
+            return self.copy(ref, ref, SS.at[s, mm], RS.at[s, mm], right if direction == 0 else left)
+        def ag_in(stage, b, k, direction):
+            s = sl(b)
+            if stage == 2:
+                n, LL, A, Bb, p, right, left, m = n2, L2, La2, Lb2, p2, r2, l2, c.m_ag2
+                at = lambda slot, part: grow(slot * L2) + part
+            else:
+                n, LL, A, Bb, p, right, left, m = n1, L, La, Lb, p1, r1, l1, c.m_ag1
+                at = lambda slot, part: base + slot * L + part
+            if k == 1:
+                row, cnt = (at(p, 0), A) if direction == 0 else (at(mod(p + 1, n), A), Bb)
+            else:
+                row, cnt = (at(mod(p - 1 - (k - 2), n), 0) if direction == 0 else at(mod(p + 2 + (k - 2), n), 0)), LL
+            ref = G.at[b, pl.ds(m16(row), cnt)]
+            mm = m + 2 * (k - 1) + direction
+            return self.copy(ref, ref, SS.at[s, mm], RS.at[s, mm], right if direction == 0 else left)
+        def ag_wait(stage, b, k):
+            for direction in (0, 1):
+                ag_copy(stage, b, k, direction).wait_send()
+                ag_in(stage, b, k, direction).wait_recv()
+        def ag_start(stage, b, k):
+            for direction in (0, 1):
+                ag_copy(stage, b, k, direction).start()
+        def pair(b):
+            s = sl(b)
+            ref = G.at[b, pl.ds(m16(base), c.S)]
+            return self.copy(ref, ref, SS.at[s, c.m_pair], RS.at[s, c.m_pair], self.partner)
+        def pair_in(b):
+            s = sl(b)
+            ref = G.at[b, pl.ds(m16(self.other + c.off), c.S)]
+            return self.copy(ref, ref, SS.at[s, c.m_pair], RS.at[s, c.m_pair], self.partner)
+
+        out = []
+        for k in range(1, h1 + 1):
+            out.append(rs_step(1, k))
+        for k in range(1, h2 + 1):
+            if k == 1:
+                out.append(lambda b: (rs_end(1)(b), rs_step(2, 1)(b)))
+            else:
+                out.append(rs_step(2, k))
+        out.append(lambda b: (rs_end(2)(b), y_send(b)))
+        out.append(lambda b: (y_sum(b), ag_start(2, b, 1)))
+        for k in range(2, h2 + 1):
+            out.append(lambda b, k=k: (ag_wait(2, b, k - 1), ag_start(2, b, k)))
+        out.append(lambda b: (ag_wait(2, b, h2), ag_start(1, b, 1)))
+        for k in range(2, h1 + 1):
+            out.append(lambda b, k=k: (ag_wait(1, b, k - 1), ag_start(1, b, k)))
+        out.append(lambda b: (ag_wait(1, b, h1), pair(b).start()))
+        out.append(lambda b: (pair(b).wait_send(), pair_in(b).wait_recv()))
+        return out
+
+def kernel(comm, K, g_hbm, o_hbm, *scratch):
+    B = comm.B
+    cs, lsem, osem = scratch[:-2], scratch[-2], scratch[-1]
+    comm.setup(cs)
+    load = lambda b: pltpu.make_async_copy(g_hbm.at[b], comm.G.at[b], lsem.at[b])
+    store = lambda b: pltpu.make_async_copy(comm.G.at[b], o_hbm.at[b], osem.at[b])
+    for b in range(B):
+        load(b).start()
+    comm.barrier()
+    phases = comm.phases()
+    nph = len(phases)
+    depth = -(-nph // K)
+    def iteration(it, _):
+        for sub in range(K):
+            for i in range(depth):
+                ph = sub + K * i
+                if ph >= nph:
+                    continue
+                b = it - i
+                @pl.when((b >= 0) & (b < B))
+                def _():
+                    if ph == 0:
+                        load(b).wait()
+                    for f in phases[ph]:
+                        f(b)
+                    if ph == nph - 1:
+                        store(b).start()
+        return 0
+    lax.fori_loop(0, B + depth - 1, iteration, 0)
+    def fin(b, _):
+        store(b).wait()
+        return 0
+    lax.fori_loop(0, B, fin, 0)
+
+def allsum(comm, K, g, vmem=66_000_000):
+    return pl.pallas_call(
+        functools.partial(kernel, comm, K),
+        out_shape=jax.ShapeDtypeStruct((comm.B, comm.TB, LANES), BF16),
+        in_specs=[pl.BlockSpec(memory_space=pl.ANY)], out_specs=pl.BlockSpec(memory_space=pl.ANY),
+        scratch_shapes=comm.scratch() + [pltpu.SemaphoreType.DMA((comm.B,)), pltpu.SemaphoreType.DMA((comm.B,))],
+        compiler_params=pltpu.CompilerParams(collective_id=0, has_side_effects=True, vmem_limit_bytes=vmem),
+    )(g)
 def matmul(a, w):
     return jnp.dot(a, w, preferred_element_type=jnp.float32).astype(jnp.bfloat16)
 
@@ -30,7 +373,32 @@
     return (w - 0.02 * step).astype(jnp.bfloat16), m, v
 
 
+TILE = 16
+COLORS = (("a", 224 * TILE, "xzy"), ("b", 224 * TILE, "yzx"), ("c", 128 * TILE, "zxy"))
+SIZES = {"x": 4, "y": 4, "z": 8}
+PARTS = 3
+
+
+def pack(g, l):
+    gate, up, down = g
+    d, f = gate.shape
+    step = f // PARTS
+    cols = lambda t: t.reshape(d, PARTS, step // LANES, LANES).transpose(1, 2, 0, 3).reshape(PARTS, -1, LANES)
+    rows = down.reshape(PARTS, step, d // LANES, LANES).transpose(0, 2, 1, 3).reshape(PARTS, -1, LANES)
+    return jnp.concatenate([cols(gate), cols(up), rows], 1)
+
+
+def unpack(s, d, f):
+    step = f // PARTS
+    n = step * d // LANES
+    cols = lambda t: t.reshape(2, PARTS, step // LANES, d, LANES).transpose(0, 3, 1, 2, 4).reshape(2, d, f)
+    rows = lambda t: t.reshape(2, PARTS, d // LANES, step, LANES).transpose(0, 1, 3, 2, 4).reshape(2, f, d)
+    return cols(s[:, :n]), cols(s[:, n : 2 * n]), rows(s[:, 2 * n :])
+
+
 def solution(mesh):
+    comm = Comm(SIZES, COLORS, 2 * PARTS, 4)
+
     def step(x, dy, *arrays):
         weights, m, v = (arrays[i : i + 3] for i in (0, 3, 6))
         layers = weights[0].shape[0]
@@ -38,12 +406,15 @@
         for number in range(layers):
             kept.append(h)
             h = layer(h, {name: w[number] for name, w in zip(NAMES, weights, strict=True)})
-        by_h, summed = dy[0], [None] * layers
+        by_h, terms = dy[0], [None] * layers
         for number in reversed(range(layers)):
             _, back = jax.vjp(lambda w, h: layer(h, w), {name: w[number] for name, w in zip(NAMES, weights, strict=True)}, kept[number])
             by_w, by_h = back(by_h)
-            summed[number] = [lax.psum(by_w[name], "dp") for name in NAMES]
-        gradients = [jnp.stack([summed[number][i] for number in range(layers)]).astype(jnp.float32) for i in range(3)]
+            terms[number] = pack([by_w[name] for name in NAMES], number)
+        summed = allsum(comm, 4, jnp.concatenate([terms[1], terms[0]], 0))
+        summed = jnp.concatenate([summed[PARTS:], summed[:PARTS]], 0)
+        d, f = weights[0].shape[1:]
+        gradients = [g.astype(jnp.float32) for g in unpack(summed, d, f)]
         new = [adamw(w.astype(jnp.float32), m, v, g) for w, m, v, g in zip(weights, m, v, gradients, strict=True)]
         return tuple(one[which] for which in range(3) for one in new)
 

time: 698 us -> 753 us (1.079)
  waiting for transfers between devices: 415 us -> 0 us
  local copies, waits for them, and re-layouts: 4.57 us -> 203 us
  Pallas kernels: 0 us -> 196 us
  other arithmetic: 101 us -> 192 us
  between operations: 14.5 us -> 1.2 us
    psum x1 -> x0, waiting for transfers between devices: 415 us -> none  [step(): summed[number] = [lax.psum(by_w[name], 'dp') for name in NAMES]]
    pallas_call x0 -> x1, Pallas kernels: none -> 196 us  [allsum(): pl.pallas_call(functools.partial(kernel, comm, K), out_shape=jax.ShapeDty...]
    convert_element_type x0 -> x6, local copies, waits for them, and re-layouts: none -> 130 us  [step(): gradients = [g.astype(jnp.float32) for g in unpack(summed, d, f)]]
    concatenate x0 -> x2, other arithmetic: none -> 50.6 us  [the longest x1 35.6 us: step(): summed = allsum(comm, 4, jnp.concatenate([terms[1], terms[0]], 0))]
    reshape x0 -> x6, local copies, waits for them, and re-layouts: none -> 34.3 us  [the longest x2 21.5 us: pack(): down.reshape(PARTS, step, d // LANES, LANES).transpose(0, 2, 1, 3)]
    convert_element_type x0 -> x2, other arithmetic: none -> 25.7 us  [step(): gradients = [g.astype(jnp.float32) for g in unpack(summed, d, f)]]
    slice x0 -> x1, local copies, waits for them, and re-layouts: none -> 16 us  [step(): summed = jnp.concatenate([summed[PARTS:], summed[:PARTS]], 0)]
    convert_element_type x2, other arithmetic: 99.7 us -> 114 us  [adamw(): return ((w - 0.02 * step).astype(jnp.bfloat16), m, v)]
  transfers between devices with their start and end apart: 1 -> 0, of which waited for: 1 -> 0; matrix products, arithmetic and copies ran while one was open for 0% -> 0% of each run, Pallas kernels for 0% -> 0%
where the time goes in v1:
time: 753 us; the launch traced here: 744 us
  local copies, waits for them, and re-layouts  203 us (27%)
  Pallas kernels  196 us (26%)
  other arithmetic  192 us (25%)
  matrix products  152 us (20%)
    pallas_call x1, Pallas kernels, allsum(): pl.pallas_call(functools.partial(kernel, comm, K), out_shape=jax.ShapeDty...  196 us
    convert_element_type x6, local copies, waits for them, and re-layouts, step(): gradients = [g.astype(jnp.float32) for g in unpack(summed, d, f)]  130 us
    convert_element_type x2, other arithmetic, adamw(): return ((w - 0.02 * step).astype(jnp.bfloat16), m, v)  114 us
    dot_general x5, matrix products, layer(): gate = jnp.dot(a, w['w_gate'], preferred_element_type=jnp.float32)  53.6 us
    dot_general x5, matrix products, layer(): up = jnp.dot(a, w['w_up'], preferred_element_type=jnp.float32)  50.6 us
    dot_general x5, matrix products, matmul(): jnp.dot(a, w, preferred_element_type=jnp.float32).astype(jnp.bfloat16)  47.5 us
    concatenate x1, other arithmetic, step(): summed = allsum(comm, 4, jnp.concatenate([terms[1], terms[0]], 0))  35.6 us
    convert_element_type x2, other arithmetic, step(): gradients = [g.astype(jnp.float32) for g in unpack(summed, d, f)]  25.7 us

profile of v1, /device:TPU:1, one launch (start us, length us, event | category | flops | bytes accessed | tf_op | source)
XLA Modules:
  0.0 743.7 jit_solution(18306066951473323118)
XLA Ops:
  0.6 1.7 copy.31
  2.4 0.4 fusion.59
  2.8 2.7 copy.32
  5.5 9.2 %convolution_convert_fusion.1 = bf16[1024,3072]{1,0:T(8,128)(2,1)} fusion(bf16[2,3072,768]{2,1,0:T(8,128)(2,1)} %param.15, bf16[1,1024,768]{2,1,0:T(8,128)(2,1)} %param.12), kind=kOutput, calls=%fused_computation.60 | convolution fusion | flops 4834983936 | bytes 12582912 | tf_op jit(solution)/shard_map/transpose(jvp())/dot_general | solution.py:353
  14.7 10.6 %fusion.48 = f32[1024,3072]{1,0:T(8,128)} fusion(bf16[2,768,3072]{2,1,0:T(8,128)(2,1)} %param.13, bf16[1,1024,768]{2,1,0:T(8,128)(2,1)S(1)} %copy-done.3, f32[1024]{0:T(1024)S(1)} %add_rsqrt_fusion), kind=kOutput, calls=%fused_computation.84 | convolution fusion | flops 4834197504 | bytes 18878464 | tf_op jit(solution)/shard_map/dot_general | solution.py:364
  25.4 12.4 %multiply_convert_fusion.1 = (bf16[1024,3072]{1,0:T(8,128)(2,1)}, f32[1024,3072]{1,0:T(8,128)}) fusion(f32[1024,3072]{1,0:T(8,128)} %fusion.48, bf16[2,768,3072]{2,1,0:T(8,128)(2,1)S(1)} %bitcast.124, bf16[1,1024,768]{2,1,0:T(8,128)(2,1)S(1)} %copy-done.3, f32[1024]{0:T(1024)S(1)} %add_rsqrt_fusion), kind=kOutput, calls=%fused_computation.49 | convolution fusion | flops 4853071872 | bytes 37752832 | tf_op jit(solution)/shard_map/dot_general | solution.py:365
  37.8 8.8 %fusion.63 = (f32[1024]{0:T(1024)S(1)}, bf16[1024,768]{0,1:T(8,128)(2,1)S(1)}) fusion(bf16[1024,3072]{1,0:T(8,128)(2,1)} %get-tuple-element.23, bf16[2,3072,768]{2,1,0:T(8,128)(2,1)} %param.15, bf16[1,1024,768]{1,2,0:T(8,128)(2,1)S(1)} %copy.31), kind=kOutput, calls=%fused_computation.102 | convolution fusion | flops 4835769344 | bytes 14159872 | tf_op jit(solution)/shard_map/dot_general | solution.py:353
  46.6 8.6 %fusion.40 = f32[1024,3072]{1,0:T(8,128)} fusion(bf16[2,768,3072]{2,1,0:T(8,128)(2,1)S(1)} %bitcast.124, bf16[1024,768]{0,1:T(8,128)(2,1)S(1)} %get-tuple-element.26, f32[1024]{0:T(1024)S(1)} %fusion.99), kind=kOutput, calls=%fused_computation.76 | convolution fusion | flops 4834197504 | bytes 18878464 | tf_op jit(solution)/shard_map/jvp()/dot_general | solution.py:365
  55.1 18.4 %fusion.14 = (bf16[1024,3072]{1,0:T(8,128)(2,1)}, f32[1024,3072]{1,0:T(8,128)}) fusion(f32[1024,3072]{1,0:T(8,128)} %fusion.40, bf16[1024,3072]{1,0:T(8,128)(2,1)} %convolution_convert_fusion.1, bf16[2,768,3072]{2,1,0:T(8,128)(2,1)} %param.13, bf16[1024,768]{0,1:T(8,128)(2,1)S(1)} %get-tuple-element.26, f32[1024]{0:T(1024)S(1)} %fusion.99), kind=kOutput, calls=%fused_computation.40 | convolution fusion | flops 4871946240 | bytes 44044288 | tf_op jit(solution)/shard_map/jvp()/dot_general | solution.py:364
  73.5 13.1 %fusion.32 = bf16[3072,768]{1,0:T(8,128)(2,1)} fusion(f32[1024,3072]{1,0:T(8,128)} %fusion.40, bf16[1,1024,768]{2,1,0:T(8,128)(2,1)S(1)} %copy-done.4, f32[1024,3072]{1,0:T(8,128)} %get-tuple-element.28), kind=kOutput, calls=%fused_computation.68 | convolution fusion | flops 4853071872 | bytes 31457280 | tf_op jit(solution)/shard_map/transpose(jvp())/dot_general | solution.py:353
  86.6 10.8 %reshape.116 = bf16[3,1024,6,128]{3,2,1,0:T(8,128)(2,1)} reshape(bf16[3072,768]{1,0:T(8,128)(2,1)} %fusion.32) | data formatting | bytes 9437184 | tf_op jit(solution)/shard_map/reshape | solution.py:387
  97.4 5.9 copy.35
  103.3 10.9 %fusion.79 = bf16[1024,768]{0,1:T(8,128)(2,1)S(1)} fusion(bf16[2,768,3072]{2,1,0:T(8,128)(2,1)} %param.14, bf16[1024,3072]{1,0:T(8,128)(2,1)} %convolution_convert_fusion.1, f32[1024,3072]{1,0:T(8,128)} %get-tuple-element.28), kind=kOutput, calls=%fused_computation.112 | convolution fusion | flops 4851499008 | bytes 25165824 | tf_op jit(solution)/shard_map/transpose(jvp())/dot_general | solution.py:365
  114.2 9.4 %fusion.67 = bf16[96,8,24,128]{3,1,2,0:T(8,128)(2,1)S(1)} fusion(bf16[1024,3072]{1,0:T(8,128)(2,1)} %convolution_convert_fusion.1, bf16[1024,768]{0,1:T(8,128)(2,1)S(1)} %get-tuple-element.26, f32[1024]{0:T(1024)S(1)} %fusion.99, f32[1024,3072]{1,0:T(8,128)} %get-tuple-element.28), kind=kOutput, calls=%fused_computation.107 | convolution fusion | flops 4855431168 | bytes 25169920 | tf_op jit(solution)/shard_map/transpose(jvp())/dot_general | solution.py:365
  123.6 1.4 copy.43
  125.0 0.0 slice-start.5
  125.0 3.1 copy.34
  128.2 0.1 slice-done.5
  128.4 5.3 fusion.65
  133.7 5.5 fusion.68
  139.2 1.4 copy.42
  140.6 3.4 copy.33
  144.0 1.1 fusion.83
  145.2 0.0 slice-done.9
  145.2 6.9 convolution_convert_fusion.2
  152.1 10.8 %reshape.122 = bf16[3,1024,6,128]{3,2,1,0:T(8,128)(2,1)} reshape(bf16[3072,768]{1,0:T(8,128)(2,1)} %convolution_convert_fusion.2) | data formatting | bytes 9437184 | tf_op jit(solution)/shard_map/reshape | solution.py:387
  162.8 5.9 copy.38
  168.7 9.5 %convolution_convert_fusion = bf16[1024,3072]{1,0:T(8,128)(2,1)} fusion(bf16[1024,768]{0,1:T(8,128)(2,1)S(1)} %fusion.83, bf16[2,3072,768]{2,1,0:T(8,128)(2,1)} %param.15), kind=kOutput, calls=%fused_computation.59 | convolution fusion | flops 4834983936 | bytes 12582912 | tf_op jit(solution)/shard_map/transpose(jvp())/dot_general | solution.py:353
  178.2 13.8 %fusion.69 = bf16[96,8,24,128]{3,1,2,0:T(8,128)(2,1)S(1)} fusion(f32[1024,3072]{1,0:T(8,128)} %fusion.48, f32[1024,3072]{1,0:T(8,128)} %get-tuple-element.24, bf16[1024,3072]{1,0:T(8,128)(2,1)} %convolution_convert_fusion, bf16[1,1024,768]{1,2,0:T(8,128)(2,1)S(1)} %copy-done.1, f32[1024]{0:T(1024)S(1)} %copy-done.8), kind=kOutput, calls=%fused_computation.109 | convolution fusion | flops 4871159808 | bytes 37752832 | tf_op jit(solution)/shard_map/transpose(jvp())/dot_general | solution.py:364
  192.1 9.3 %fusion.66 = bf16[96,8,24,128]{3,1,2,0:T(8,128)(2,1)S(1)} fusion(bf16[1024,3072]{1,0:T(8,128)(2,1)} %convolution_convert_fusion, f32[1024,3072]{1,0:T(8,128)} %fusion.48, bf16[1,1024,768]{1,2,0:T(8,128)(2,1)S(1)} %copy-done.1, f32[1024]{0:T(1024)S(1)} %copy-done.8), kind=kOutput, calls=%fused_computation.106 | convolution fusion | flops 4855431168 | bytes 25169920 | tf_op jit(solution)/shard_map/transpose(jvp())/dot_general | solution.py:365
  201.4 1.4 copy.45
  202.8 3.2 copy.37
  206.0 1.4 copy.44
  207.4 3.2 copy.36
  210.5 35.6 %maximum_maximum_fusion.g_hbm = bf16[6,18432,128]{2,1,0:T(8,128)(2,1)} fusion(bf16[3,6144,128]{2,1,0:T(8,128)(2,1)} %bitcast.130, bf16[3,6144,128]{2,1,0:T(8,128)(2,1)} %bitcast.127, bf16[3,6144,128]{2,1,0:T(8,128)(2,1)} %bitcast.128, bf16[3,6144,128]{2,1,0:T(8,128)(2,1)} %bitcast.129, bf16[3,6144,128]{2,1,0:T(8,128)(2,1)} %bitcast.125, ...), kind=kLoop, calls=%fused_computation.4 | loop fusion | flops 169869312 | bytes 56623104 | tf_op jit(solution)/shard_map/concatenate | solution.py:414
  246.2 196.2 %shard_map.178 = bf16[6,18432,128]{2,1,0:T(8,128)(2,1)} custom-call(bf16[6,18432,128]{2,1,0:T(8,128)(2,1)} %maximum_maximum_fusion.g_hbm), custom_call_target="tpu_custom_call" | custom-call | tf_op jit(solution)/shard_map/pallas_call | solution.py:345
  442.4 16.0 %fusion.108 = (bf16[3,18432,128]{2,1,0:T(8,128)(2,1)S(1)}, bf16[3,18432,128]{2,1,0:T(8,128)(2,1)}) fusion(bf16[6,18432,128]{2,1,0:T(8,128)(2,1)} %shard_map.178), kind=kLoop, calls=%fused_computation.125 | loop fusion | bytes 56623104 | tf_op jit(solution)/shard_map/slice | solution.py:415
  458.3 15.0 %pad_maximum_fusion = (bf16[6,6144,128]{2,1,0:T(8,128)(2,1)}, bf16[6,6144,128]{2,1,0:T(8,128)(2,1)}, bf16[6,6144,128]{2,1,0:T(8,128)(2,1)}) fusion(bf16[3,18432,128]{2,1,0:T(8,128)(2,1)S(1)} %get-tuple-element.21, bf16[3,18432,128]{2,1,0:T(8,128)(2,1)} %get-tuple-element.22), kind=kLoop, calls=%fused_computation.54 | loop fusion | flops 56623104 | bytes 56623104 | tf_op jit(solution)/shard_map/concatenate | solution.py:415
  473.3 12.9 %convert_bitcast_fusion.1 = f32[2,768,3,8,128]{4,1,3,2,0:T(8,128)} fusion(bf16[2,3,8,768,128]{4,3,2,1,0:T(8,128)(2,1)} %bitcast.119), kind=kLoop, calls=%fused_computation.30 | loop fusion | flops 4718592 | bytes 28311552 | tf_op jit(solution)/shard_map/convert_element_type | solution.py:417
  486.2 25.2 %copy.39 = f32[2,768,3,8,128]{4,3,2,1,0:T(8,128)} copy(f32[2,768,3,8,128]{4,1,3,2,0:T(8,128)} %convert_bitcast_fusion.1) | data formatting | bytes 37748736 | tf_op jit(solution)/shard_map/convert_element_type | solution.py:417
  511.4 20.4 %reshape.124 = f32[2,768,3072]{2,1,0:T(8,128)} reshape(f32[2,768,3,8,128]{4,3,2,1,0:T(8,128)} %copy.39) | data formatting | bytes 37748736 | tf_op jit(solution)/shard_map/convert_element_type | solution.py:417
  531.8 14.9 %copy.47 = f32[2,3,6,1024,128]{4,2,3,1,0:T(8,128)} copy(bf16[2,3,6,1024,128]{4,3,2,1,0:T(8,128)(2,1)} %bitcast.120) | data formatting | bytes 28311552 | tf_op jit(solution)/shard_map/convert_element_type | solution.py:417
  546.8 24.2 %reshape.126 = f32[2,3072,768]{2,1,0:T(8,128)} reshape(f32[2,3,1024,6,128]{4,3,2,1,0:T(8,128)} %bitcast.117) | data formatting | bytes 37748736 | tf_op jit(solution)/shard_map/convert_element_type | solution.py:417
  571.0 12.9 %convert_bitcast_fusion = f32[2,768,3,8,128]{4,1,3,2,0:T(8,128)} fusion(bf16[2,3,8,768,128]{4,3,2,1,0:T(8,128)(2,1)} %bitcast.118), kind=kLoop, calls=%fused_computation.29 | loop fusion | flops 4718592 | bytes 28311552 | tf_op jit(solution)/shard_map/convert_element_type | solution.py:417
  583.9 25.2 %copy.40 = f32[2,768,3,8,128]{4,3,2,1,0:T(8,128)} copy(f32[2,768,3,8,128]{4,1,3,2,0:T(8,128)} %convert_bitcast_fusion) | data formatting | bytes 37748736 | tf_op jit(solution)/shard_map/convert_element_type | solution.py:417
  609.1 20.4 %reshape.125 = f32[2,768,3072]{2,1,0:T(8,128)} reshape(f32[2,768,3,8,128]{4,3,2,1,0:T(8,128)} %copy.40) | data formatting | bytes 37748736 | tf_op jit(solution)/shard_map/convert_element_type | solution.py:417
  629.5 39.2 %fusion.8 = (bf16[2,3072,768]{2,1,0:T(8,128)(2,1)}, f32[2,3072,768]{2,1,0:T(8,128)}, f32[2,3072,768]{2,1,0:T(8,128)}) fusion(bf16[2,3072,768]{2,1,0:T(8,128)(2,1)} %param.15, f32[2,3072,768]{2,1,0:T(8,128)} %reshape.126, f32[2,3072,768]{2,1,0:T(8,128)} %param.21, f32[2,3072,768]{2,1,0:T(8,128)} %param.18), kind=kLoop, calls=%fused_computation.25 | loop fusion | flops 70778880 | bytes 113246208 | tf_op jit(solution)/shard_map/convert_element_type | solution.py:373
  668.7 74.7 %fusion.2 = (bf16[2,768,3072]{2,1,0:T(8,128)(2,1)}, f32[2,768,3072]{2,1,0:T(8,128)}, f32[2,768,3072]{2,1,0:T(8,128)}, bf16[2,768,3072]{2,1,0:T(8,128)(2,1)}, f32...) fusion(bf16[2,768,3072]{2,1,0:T(8,128)(2,1)} %param.13, f32[2,768,3072]{2,1,0:T(8,128)} %reshape.124, ...), kind=kLoop, calls=%fused_computation.19 | loop fusion | flops 141557760 | bytes 226492416 | tf_op jit(solution)/shard_map/convert_element_type | solution.py:373
  (42 shorter events, 0.1 us)
Async XLA Ops:
  2.4 35.4 %copy-start = (bf16[1,1024,768]{1,2,0:T(8,128)(2,1)}, bf16[1,1024,768]{1,2,0:T(8,128)(2,1)S(1)}, u32[]{:S(2)}) copy-start(bf16[1,1024,768]{1,2,0:T(8,128)(2,1)S(1)} %copy.31) | copy-start | bytes 4718596
  2.7 22.6 %copy-start.7 = (f32[1024]{0:T(1024)}, f32[1024]{0:T(1024)S(1)}, u32[]{:S(2)}) copy-start(f32[1024]{0:T(1024)S(1)} %add_rsqrt_fusion) | copy-start | bytes 12292
  5.5 9.2 %copy-start.3 = (bf16[1,1024,768]{2,1,0:T(8,128)(2,1)S(1)}, bf16[1,1024,768]{2,1,0:T(8,128)(2,1)}, u32[]{:S(2)}) copy-start(bf16[1,1024,768]{2,1,0:T(8,128)(2,1)} %param.11) | copy-start | bytes 4718596
  5.5 19.9 %slice-start = ((s8[9437184]{0:T(1024)(128)(4,1)}), s8[4194304]{0:T(1024)(128)(4,1)S(1)}, s32[]{:S(2)}) async-start(s8[9437184]{0:T(1024)(128)(4,1)} %bitcast.123), calls=%async_computation | async-start | bytes 8388608
  5.5 19.9 %slice-start.1 = ((s8[9437184]{0:T(1024)(128)(4,1)}), s8[4194304]{0:T(1024)(128)(4,1)S(1)}, s32[]{:S(2)}) async-start(s8[9437184]{0:T(1024)(128)(4,1)} %bitcast.123), calls=%async_computation.1 | async-start | bytes 8388608
  14.7 10.6 %slice-start.2 = ((s8[9437184]{0:T(1024)(128)(4,1)}), s8[1048576]{0:T(1024)(128)(4,1)S(1)}, s32[]{:S(2)}) async-start(s8[9437184]{0:T(1024)(128)(4,1)} %bitcast.123), calls=%async_computation.2 | async-start | bytes 2097152
  46.6 8.6 %copy-start.5 = (f32[1024]{0:T(1024)}, f32[1024]{0:T(1024)S(1)}, u32[]{:S(2)}) copy-start(f32[1024]{0:T(1024)S(1)} %get-tuple-element.25) | copy-start | bytes 12292
  55.1 18.4 %copy-start.4 = (bf16[1,1024,768]{2,1,0:T(8,128)(2,1)S(1)}, bf16[1,1024,768]{2,1,0:T(8,128)(2,1)}, u32[]{:S(2)}) copy-start(bf16[1,1024,768]{2,1,0:T(8,128)(2,1)} %param.12) | copy-start | bytes 4718596
  103.3 24.9 %slice-start.6 = ((s8[6291456]{0:T(1024)(128)(4,1)}), s8[4194304]{0:T(1024)(128)(4,1)S(1)}, s32[]{:S(2)}) async-start(s8[6291456]{0:T(1024)(128)(4,1)} %bitcast.137), calls=%async_computation.6 | async-start | bytes 8388608
  114.2 14.0 %slice-start.7 = ((s8[6291456]{0:T(1024)(128)(4,1)}), s8[2097152]{0:T(1024)(128)(4,1)S(1)}, s32[]{:S(2)}) async-start(s8[6291456]{0:T(1024)(128)(4,1)} %bitcast.137), calls=%async_computation.7 | async-start | bytes 4194304
  123.6 4.6 slice-start.3
  123.6 4.6 slice-start.4
  125.0 3.3 slice-start.5
  139.2 4.8 copy-start.6
  139.2 4.8 copy-start.2
  140.6 4.6 slice-start.8
  140.6 4.6 slice-start.9
  168.7 9.5 %copy-start.1 = (bf16[1,1024,768]{1,2,0:T(8,128)(2,1)S(1)}, bf16[1,1024,768]{1,2,0:T(8,128)(2,1)}, u32[]{:S(2)}) copy-start(bf16[1,1024,768]{1,2,0:T(8,128)(2,1)} %copy-done) | copy-start | bytes 4718596
  168.7 9.5 %copy-start.8 = (f32[1024]{0:T(1024)S(1)}, f32[1024]{0:T(1024)}, u32[]{:S(2)}) copy-start(f32[1024]{0:T(1024)} %copy-done.7) | copy-start | bytes 12292

commit v2 on v1

--- a/solution.py
+++ b/solution.py
@@ -1,25 +1,22 @@
 import functools
-
 import jax
 import jax.numpy as jnp
 from jax import lax
 from jax.experimental import pallas as pl
 from jax.experimental.pallas import tpu as pltpu
 from jax.sharding import PartitionSpec as P
-
-NAMES = ("w_gate", "w_up", "w_down")
 MESH = pl.DeviceIdType.MESH
 F32, BF16 = jnp.float32, jnp.bfloat16
 LANES = 128
 
-def chunk_of(n, cap=128):
+def chunk_of(n, cap=256):
     best = 16
     for c in range(16, cap + 1, 16):
         if n % c == 0:
             best = c
     return best
 
-def over_rows(n, body, cap=128):
+def over_rows(n, body, cap=256):
     c = chunk_of(n, cap)
     if n == c:
         body(0, c)
@@ -61,15 +58,15 @@
     return pl.multiple_of(v, 16)
 
 class Comm:
-    def __init__(self, n, cfg, B, NB):
-        self.n, self.B, self.NB = n, B, NB
+    def __init__(self, n, cfg, B, NB, ND=None):
+        self.n, self.B, self.NB, self.ND = n, B, NB, ND or NB
         off, self.colors = 0, []
         for name, rows, dims in cfg:
             self.colors.append(Color(name, off, rows, dims, n)); off += rows
         self.HB, self.TB = off, 2 * off
     def scratch(self):
-        out = [pltpu.VMEM((self.B, self.TB, LANES), BF16), pltpu.VMEM((self.NB, self.HB, LANES), BF16),
-               pltpu.SemaphoreType.DMA((self.NB,)), pltpu.SemaphoreType.DMA((self.NB,))]
+        out = [pltpu.VMEM((self.B, self.TB, LANES), BF16), pltpu.VMEM((self.ND, self.HB, LANES), BF16),
+               pltpu.SemaphoreType.DMA((self.ND,)), pltpu.SemaphoreType.DMA((self.ND,))]
         for c in self.colors:
             out += c.scratch(self.NB)
         return out
@@ -113,7 +110,7 @@
         return pltpu.make_async_remote_copy(src_ref=src, dst_ref=dst, send_sem=ss, recv_sem=rs, device_id={"dp": dev}, device_id_type=MESH)
 
     def pair_copy(self, b):
-        s = lax.rem(b, self.NB)
+        s = lax.rem(b, self.ND)
         return self.copy(self.G.at[b, pl.ds(m16(self.other), self.HB)], self.D.at[s], self.ds.at[s], self.dr.at[s], self.partner)
     def phases(self):
         out = [[lambda b: self.pair_copy(b).start()], [lambda b: self.pair_copy(b).wait()]]
@@ -138,6 +135,7 @@
         base = self.mine + c.off
         dbase = c.off
         sl = lambda b: lax.rem(b, NB)
+        dsl = lambda b: lax.rem(b, self.ND)
 
         def ring(stage):
             if stage == 1:
@@ -145,11 +143,11 @@
             return dict(n=n2, h=h2, L=L2, La=La2, Lb=Lb2, p=p2, right=r2, left=l2, R=R2, m=c.m_rs2)
         def local(stage, b, row, k):
             if stage == 1:
-                return G[b, pl.ds(m16(base + row), k), :].astype(F32) + D[sl(b), pl.ds(m16(dbase + row), k), :].astype(F32)
+                return G[b, pl.ds(m16(base + row), k), :].astype(F32) + D[dsl(b), pl.ds(m16(dbase + row), k), :].astype(F32)
             return O1[sl(b), pl.ds(m16(row), k), :] + R1[sl(b), pl.ds(m16(2 * (h1 - 1) * L + row), k), :].astype(F32)
         def staged(stage, b, row, k):
             if stage == 1:
-                return D.at[sl(b), pl.ds(m16(dbase + row), k)]
+                return D.at[dsl(b), pl.ds(m16(dbase + row), k)]
             return O1b.at[sl(b), pl.ds(m16(row), k)]
         def rs_copy(stage, b, k, direction):
             g = ring(stage)
@@ -185,9 +183,10 @@
                     def send_part(lo, cnt):
                         def body(i, kk):
                             v = total(slot * LL + lo + i, lo + i, kk)
-                            ref = D if stage == 1 else O1b
-                            o = (dbase if stage == 1 else 0) + slot * LL + lo + i
-                            ref[s, pl.ds(m16(o), kk), :] = v.astype(BF16)
+                            if stage == 1:
+                                D[dsl(b), pl.ds(m16(dbase + slot * LL + lo + i), kk), :] = v.astype(BF16)
+                            else:
+                                O1b[s, pl.ds(m16(slot * LL + lo + i), kk), :] = v.astype(BF16)
                         over_rows(cnt, body)
                     def keep_part(lo, cnt, to):
                         ref = O1 if stage == 1 else O2
@@ -307,119 +306,259 @@
         out.append(lambda b: (pair(b).wait_send(), pair_in(b).wait_recv()))
         return out
 
-def kernel(comm, K, g_hbm, o_hbm, *scratch):
+
+TOK, DIM, FF = 1024, 768, 3072
+TF = 256
+NT = FF // TF
+PARTS = 3
+K = NT // PARTS
+HALF = 512
+
+def dot(a, b):
+    return jnp.dot(a, b, preferred_element_type=F32)
+def dot_nt(a, b):
+    return lax.dot_general(a, b, (((1,), (1,)), ((), ())), preferred_element_type=F32)
+
+OFFS = {
+    "A": [0, 1, 3, 4, 5, 6, 7, 8, 9, 10, 11, 12, 13, 14, 16, 17],
+    "B": [0, 1, 3, 4, 5, 6, 7, 8, 9, 10, 11, 12, 13, 14, 16, 17],
+    "C": [0, 1, 2, 3, 4, 6, 7, 8, 9, 10, 11, 12, 13, 14, 16, 17],
+}
+
+def mega(comm, x_hbm, dy_hbm, wg_hbm, wu_hbm, wd_hbm, o_hbm, A, AT, DY, DYT, H, ACC, TH, TG, TU, WG, WU, WD, wsem, xsem, osem, *cs):
     B = comm.B
-    cs, lsem, osem = scratch[:-2], scratch[-2], scratch[-1]
     comm.setup(cs)
-    load = lambda b: pltpu.make_async_copy(g_hbm.at[b], comm.G.at[b], lsem.at[b])
-    store = lambda b: pltpu.make_async_copy(comm.G.at[b], o_hbm.at[b], osem.at[b])
-    for b in range(B):
-        load(b).start()
+    G = comm.G
+    def wcopies(u):
+        q = lax.div(u, NT)
+        layer = lax.rem(q, 2)
+        j = lax.rem(u, NT)
+        s = lax.rem(u, 2)
+        f = pl.multiple_of(j * TF, TF)
+        return (pltpu.make_async_copy(wg_hbm.at[layer, :, pl.ds(f, TF)], WG.at[s], wsem.at[s, 0]),
+                pltpu.make_async_copy(wu_hbm.at[layer, :, pl.ds(f, TF)], WU.at[s], wsem.at[s, 1]),
+                pltpu.make_async_copy(wd_hbm.at[layer, pl.ds(f, TF), :], WD.at[s], wsem.at[s, 2]))
+    def wstart(u):
+        for c in wcopies(u):
+            c.start()
+    def wwait(u):
+        for c in wcopies(u):
+            c.wait()
+    xin = pltpu.make_async_copy(x_hbm, H, xsem.at[0])
+    xagain = pltpu.make_async_copy(x_hbm, A, xsem.at[0])
+    dyin = pltpu.make_async_copy(dy_hbm, DY, xsem.at[1])
+    xin.start(); dyin.start(); wstart(0)
     comm.barrier()
+
+    def rows_of(i, n):
+        return pl.ds(pl.multiple_of(i * n, n), n)
+    def each(n, body):
+        def step(i, _):
+            body(rows_of(i, n))
+            return 0
+        lax.fori_loop(0, TOK // n, step, 0)
+    def norm(src, r):
+        wide = src[r, :].astype(F32)
+        scale = lax.rsqrt(jnp.mean(wide * wide, -1, keepdims=True) + 1e-6)
+        return (wide * scale).astype(BF16)
+    def zero(r):
+        ACC[r, :] = jnp.zeros((r.size, DIM), F32)
+
+    xin.wait()
+    def first(r):
+        A[r, :] = norm(H, r)
+        zero(r)
+    each(128, first)
+
+    def forward(u, _):
+        s = lax.rem(u, 2)
+        wwait(u)
+        wstart(u + 1)
+        def half(r):
+            a = A[r, :]
+            gate = dot(a, WG[s])
+            up = dot(a, WU[s])
+            hid = (gate * jax.nn.sigmoid(gate) * up).astype(BF16)
+            ACC[r, :] += dot(hid, WD[s])
+        for i in range(TOK // HALF):
+            half(pl.ds(i * HALF, HALF))
+        return 0
+    lax.fori_loop(0, NT, forward, 0)
+    dyin.wait()
+    def between(r):
+        H[r, :] = (H[r, :].astype(F32) + ACC[r, :].astype(BF16).astype(F32)).astype(BF16)
+        a = norm(H, r)
+        A[r, :] = a
+        AT[:, r] = a.T
+        DYT[:, r] = DY[r, :].T
+        zero(r)
+    each(128, between)
+
+    def backward(u, t, want_input):
+        s = lax.rem(u, 2)
+        b = lax.div(t, K)
+        jt = lax.rem(t, K)
+        wwait(u)
+        @pl.when(u + 1 < 3 * NT)
+        def _():
+            wstart(u + 1)
+        for i in range(TOK // HALF):
+            r = pl.ds(i * HALF, HALF)
+            a = A[r, :]
+            gate = dot(a, WG[s])
+            up = dot(a, WU[s])
+            dh = dot_nt(DY[r, :], WD[s]).astype(BF16).astype(F32)
+            sig = jax.nn.sigmoid(gate)
+            act = gate * sig
+            TH[r, :] = (act * up).astype(BF16)
+            du = (dh * act).astype(BF16)
+            dg = (dh * up * (sig * (1.0 + gate * (1.0 - sig)))).astype(BF16)
+            TU[r, :] = du
+            TG[r, :] = dg
+            if want_input:
+                ACC[r, :] += dot_nt(dg, WG[s]) + dot_nt(du, WU[s])
+        for mat, (lhs, rhs) in enumerate(((AT, TG), (AT, TU), (DYT, TH))):
+            d = dot(lhs[...], rhs[...]).astype(BF16)
+            for k in range(TF // LANES):
+                row = (mat * (K * TF // LANES) + jt * (TF // LANES) + k) * DIM
+                G[b, pl.ds(m16(row), DIM), :] = d[:, k * LANES:(k + 1) * LANES]
+
+    def middle():
+        xagain.start()
+        def body(r):
+            da = ACC[r, :].astype(BF16).astype(F32)
+            wide = H[r, :].astype(F32)
+            scale = lax.rsqrt(jnp.mean(wide * wide, -1, keepdims=True) + 1e-6)
+            ds = jnp.sum(da * wide, -1, keepdims=True)
+            dwide = da * scale - wide * (ds * scale * scale * scale * (1.0 / DIM))
+            d = (DY[r, :].astype(F32) + dwide.astype(BF16).astype(F32)).astype(BF16)
+            DY[r, :] = d
+            DYT[:, r] = d.T
+        each(128, body)
+        xagain.wait()
+        def again(r):
+            a = norm(A, r)
+            A[r, :] = a
+            AT[:, r] = a.T
+        each(128, again)
+
+    store = lambda b: pltpu.make_async_copy(G.at[b], o_hbm.at[b], osem.at[b])
     phases = comm.phases()
-    nph = len(phases)
-    depth = -(-nph // K)
-    def iteration(it, _):
+    events = []
+    for ph, fns in enumerate(phases):
+        if ph == 0:
+            events += [(0, f) for f in fns]
+        else:
+            cols = [c.name for c in comm.colors]
+            fs = list(fns)
+            if ph == 1:
+                events.append((1, fs.pop(0)))
+            for name, f in zip(cols, fs):
+                events.append((OFFS[name][ph], f))
+    last = max(o for o, _ in events)
+    events.append((last, lambda b: store(b).start()))
+    depth = last // K + 1
+    def tick(t):
+        it = lax.div(t, K) - 1
         for sub in range(K):
-            for i in range(depth):
-                ph = sub + K * i
-                if ph >= nph:
-                    continue
-                b = it - i
-                @pl.when((b >= 0) & (b < B))
-                def _():
-                    if ph == 0:
-                        load(b).wait()
-                    for f in phases[ph]:
-                        f(b)
-                    if ph == nph - 1:
-                        store(b).start()
+            if not any(o % K == sub for o, _ in events):
+                continue
+            @pl.when(lax.rem(t, K) == sub)
+            def _():
+                for i in reversed(range(depth)):
+                    fs = [f for o, f in events if o == sub + K * i]
+                    if not fs:
+                        continue
+                    b = it - i
+                    @pl.when((b >= 0) & (b < B))
+                    def _():
+                        for f in fs:
+                            f(b)
+    def step(t, _):
+        tick(t)
+        @pl.when(t < NT)
+        def _():
+            backward(t + NT, t, True)
+        @pl.when(t == NT)
+        def _():
+            middle()
+        @pl.when((t >= NT) & (t < 2 * NT))
+        def _():
+            backward(t + NT, t, False)
         return 0
-    lax.fori_loop(0, B + depth - 1, iteration, 0)
+    lax.fori_loop(0, K * B + last + 1, step, 0)
     def fin(b, _):
         store(b).wait()
         return 0
     lax.fori_loop(0, B, fin, 0)
 
-def allsum(comm, K, g, vmem=66_000_000):
+def gradients(comm, x, dy, wg, wu, wd, vmem=66_900_000):
+    V = pltpu.VMEM
+    scratch = [V((TOK, DIM), BF16), V((DIM, TOK), BF16), V((TOK, DIM), BF16), V((DIM, TOK), BF16), V((TOK, DIM), BF16), V((TOK, DIM), F32),
+               V((TOK, TF), BF16), V((TOK, TF), BF16), V((TOK, TF), BF16),
+               V((2, DIM, TF), BF16), V((2, DIM, TF), BF16), V((2, TF, DIM), BF16),
+               pltpu.SemaphoreType.DMA((2, 3)), pltpu.SemaphoreType.DMA((2,)), pltpu.SemaphoreType.DMA((comm.B,))]
     return pl.pallas_call(
-        functools.partial(kernel, comm, K),
+        functools.partial(mega, comm),
         out_shape=jax.ShapeDtypeStruct((comm.B, comm.TB, LANES), BF16),
-        in_specs=[pl.BlockSpec(memory_space=pl.ANY)], out_specs=pl.BlockSpec(memory_space=pl.ANY),
-        scratch_shapes=comm.scratch() + [pltpu.SemaphoreType.DMA((comm.B,)), pltpu.SemaphoreType.DMA((comm.B,))],
+        in_specs=[pl.BlockSpec(memory_space=pl.ANY)] * 5, out_specs=pl.BlockSpec(memory_space=pl.ANY),
+        scratch_shapes=scratch + comm.scratch(),
         compiler_params=pltpu.CompilerParams(collective_id=0, has_side_effects=True, vmem_limit_bytes=vmem),
-    )(g)
-def matmul(a, w):
-    return jnp.dot(a, w, preferred_element_type=jnp.float32).astype(jnp.bfloat16)
-
-
-def normed(h):
-    wide = h.astype(jnp.float32)
-    scale = lax.rsqrt(jnp.mean(wide**2, -1, keepdims=True) + 1e-6)
-    return (wide * scale).astype(jnp.bfloat16)
-
-
-def layer(h, w):
-    a = normed(h)
-    gate = jnp.dot(a, w["w_gate"], preferred_element_type=jnp.float32)
-    up = jnp.dot(a, w["w_up"], preferred_element_type=jnp.float32)
-    return h + matmul((jax.nn.silu(gate) * up).astype(jnp.bfloat16), w["w_down"])
-
-
-def adamw(w, m, v, g):
-    m = 0.9 * m + 0.1 * g
-    v = 0.95 * v + 0.05 * g * g
-    step = m * lax.rsqrt(v + 1e-8) + 0.1 * w
-    return (w - 0.02 * step).astype(jnp.bfloat16), m, v
-
-
+    )(x, dy, wg, wu, wd)
+
+def adam_kernel(turned, w, m, v, *refs):
+    gs, (w2, m2, v2) = refs[:-3], refs[-3:]
+    for k, g in enumerate(gs):
+        gv = g[0].astype(F32)
+        if turned:
+            gv = gv.T
+            at = (0, pl.ds(k * LANES, LANES), slice(None))
+        else:
+            at = (0, slice(None), pl.ds(k * LANES, LANES))
+        mm = 0.9 * m[at] + 0.1 * gv
+        vv = 0.95 * v[at] + 0.05 * gv * gv
+        ww = w[at].astype(F32)
+        step = mm * lax.rsqrt(vv + 1e-8) + 0.1 * ww
+        w2[at] = (ww - 0.02 * step).astype(BF16)
+        m2[at] = mm
+        v2[at] = vv
+
+def adam(which, w, m, v, g, c=2):
+    turned = which == 2
+    wide = c * LANES
+    per = FF // PARTS // wide
+    if turned:
+        spec = pl.BlockSpec((1, wide, DIM), lambda l, i: (l, i, 0))
+    else:
+        spec = pl.BlockSpec((1, DIM, wide), lambda l, i: (l, 0, i))
+    def gspec(k):
+        def index(l, i):
+            return ((1 - l) * PARTS + i // per, which * (FF // PARTS // LANES) + (i % per) * c + k, 0)
+        return pl.BlockSpec((1, DIM, LANES), index)
+    return pl.pallas_call(
+        functools.partial(adam_kernel, turned),
+        grid=(2, FF // wide),
+        out_shape=(jax.ShapeDtypeStruct(w.shape, BF16), jax.ShapeDtypeStruct(m.shape, F32), jax.ShapeDtypeStruct(v.shape, F32)),
+        in_specs=[spec] * 3 + [gspec(k) for k in range(c)], out_specs=(spec,) * 3,
+        compiler_params=pltpu.CompilerParams(vmem_limit_bytes=60_000_000),
+    )(w, m, v, *([g] * c))
 TILE = 16
-COLORS = (("a", 224 * TILE, "xzy"), ("b", 224 * TILE, "yzx"), ("c", 128 * TILE, "zxy"))
+COLORS = (("A", 224 * TILE, "xzy"), ("B", 224 * TILE, "yzx"), ("C", 128 * TILE, "zxy"))
 SIZES = {"x": 4, "y": 4, "z": 8}
-PARTS = 3
-
-
-def pack(g, l):
-    gate, up, down = g
-    d, f = gate.shape
-    step = f // PARTS
-    cols = lambda t: t.reshape(d, PARTS, step // LANES, LANES).transpose(1, 2, 0, 3).reshape(PARTS, -1, LANES)
-    rows = down.reshape(PARTS, step, d // LANES, LANES).transpose(0, 2, 1, 3).reshape(PARTS, -1, LANES)
-    return jnp.concatenate([cols(gate), cols(up), rows], 1)
-
-
-def unpack(s, d, f):
-    step = f // PARTS
-    n = step * d // LANES
-    cols = lambda t: t.reshape(2, PARTS, step // LANES, d, LANES).transpose(0, 3, 1, 2, 4).reshape(2, d, f)
-    rows = lambda t: t.reshape(2, PARTS, d // LANES, step, LANES).transpose(0, 1, 3, 2, 4).reshape(2, f, d)
-    return cols(s[:, :n]), cols(s[:, n : 2 * n]), rows(s[:, 2 * n :])
+def make_comm():
+    return Comm(SIZES, COLORS, 2 * PARTS, 2, 3)
+
+def train_step(comm, x, dy, *arrays):
+    weights, m, v = (arrays[i:i + 3] for i in (0, 3, 6))
+    g = gradients(comm, x[0], dy[0], *weights)
+    new = [adam(i, weights[i], m[i], v[i], g) for i in range(3)]
+    return tuple(one[which] for which in range(3) for one in new)
 
 
 def solution(mesh):
-    comm = Comm(SIZES, COLORS, 2 * PARTS, 4)
-
-    def step(x, dy, *arrays):
-        weights, m, v = (arrays[i : i + 3] for i in (0, 3, 6))
-        layers = weights[0].shape[0]
-        h, kept = x[0], []
-        for number in range(layers):
-            kept.append(h)
-            h = layer(h, {name: w[number] for name, w in zip(NAMES, weights, strict=True)})
-        by_h, terms = dy[0], [None] * layers
-        for number in reversed(range(layers)):
-            _, back = jax.vjp(lambda w, h: layer(h, w), {name: w[number] for name, w in zip(NAMES, weights, strict=True)}, kept[number])
-            by_w, by_h = back(by_h)
-            terms[number] = pack([by_w[name] for name in NAMES], number)
-        summed = allsum(comm, 4, jnp.concatenate([terms[1], terms[0]], 0))
-        summed = jnp.concatenate([summed[PARTS:], summed[:PARTS]], 0)
-        d, f = weights[0].shape[1:]
-        gradients = [g.astype(jnp.float32) for g in unpack(summed, d, f)]
-        new = [adamw(w.astype(jnp.float32), m, v, g) for w, m, v, g in zip(weights, m, v, gradients, strict=True)]
-        return tuple(one[which] for which in range(3) for one in new)
-
+    comm = make_comm()
     return jax.shard_map(
-        step,
+        functools.partial(train_step, comm),
         mesh=mesh,
         in_specs=(P(("rep", "dp"), None, None),) * 2 + (P(None, None, None),) * 9,
         out_specs=(P("rep", None, None),) * 9,

time: 753 us -> 361 us (0.48); the launches traced: 744 us -> 360 us
  local copies, waits for them, and re-layouts: 203 us -> 0 us
  other arithmetic: 192 us -> 0 us
  Pallas kernels: 196 us -> 360 us
  matrix products: 152 us -> 0 us
    pallas_call x1 -> x4, Pallas kernels: 196 us -> 360 us  [the longest x1 235 us: gradients(): pl.pallas_call(functools.partial(mega, comm), out_shape=jax.ShapeDtypeStr...]
    dot_general x15 -> x0, matrix products: 152 us -> none  [the longest x5 53.6 us: layer(): gate = jnp.dot(a, w['w_gate'], preferred_element_type=jnp.float32)]
    convert_element_type x4 -> x0, other arithmetic: 140 us -> none  [the longest x2 114 us: adamw(): return ((w - 0.02 * step).astype(jnp.bfloat16), m, v)]
    convert_element_type x6 -> x0, local copies, waits for them, and re-layouts: 130 us -> none  [step(): gradients = [g.astype(jnp.float32) for g in unpack(summed, d, f)]]
    concatenate x2 -> x0, other arithmetic: 50.6 us -> none  [the longest x1 35.6 us: step(): summed = allsum(comm, 4, jnp.concatenate([terms[1], terms[0]], 0))]
    reshape x6 -> x0, local copies, waits for them, and re-layouts: 34.3 us -> none  [the longest x2 21.5 us: pack(): down.reshape(PARTS, step, d // LANES, LANES).transpose(0, 2, 1, 3)]
    slice x1 -> x0, local copies, waits for them, and re-layouts: 16 us -> none  [step(): summed = jnp.concatenate([summed[PARTS:], summed[:PARTS]], 0)]
    transpose x2 -> x0, local copies, waits for them, and re-layouts: 11.8 us -> none  [pack(): down.reshape(PARTS, step, d // LANES, LANES).transpose(0, 2, 1, 3)]
where the time goes in v2:
time: 361 us; the launch traced here: 360 us
  Pallas kernels  360 us (100%)
    pallas_call x1, Pallas kernels, gradients(): pl.pallas_call(functools.partial(mega, comm), out_shape=jax.ShapeDtypeStr...  235 us
    pallas_call x3, Pallas kernels, adam(): pl.pallas_call(functools.partial(adam_kernel, turned), grid=(2, FF // wid...  125 us

profile of v2, /device:TPU:1, one launch (start us, length us, event | category | flops | bytes accessed | tf_op | source)
XLA Modules:
  0.0 360.5 jit_solution(8722109757974960790)
XLA Ops:
  0.6 234.7 %shard_map.178.refs_0_.refs_1_ = bf16[6,18432,128]{2,1,0:T(8,128)(2,1)} custom-call(bf16[1024,768]{1,0:T(8,128)(2,1)} %bitcast.2, bf16[1024,768]{1,0:T(8,128)(2,1)} %bitcast.3, bf16[2,768,3072]{2,1,0:T(8,128)(2,1)} %w.3, bf16[2,768,3072]{2,1,0:T(8,128)(2,1)} %w.4, bf16[2,3072,768]{2,1,0:T(8,128)(2,1)} %w.5), custom_call_target="tpu_custom_call" | custom-call | tf_op jit(solution)/shard_map/pallas_call | solution.py:501
  235.4 43.1 %shard_map.181 = (bf16[2,3072,768]{2,1,0:T(8,128)(2,1)}, f32[2,3072,768]{2,1,0:T(8,128)}, f32[2,3072,768]{2,1,0:T(8,128)}) custom-call(bf16[2,3072,768]{2,1,0:T(8,128)(2,1)} %w.5, f32[2,3072,768]{2,1,0:T(8,128)} %m.5, f32[2,3072,768]{2,1,0:T(8,128)} %v.5, bf16[6,18432,128]{2,1,0:T(8,128)(2,1)} %shard_map.178.refs_0_.refs_1_, ...), custom_call_target="tpu_custom_call" | custom-call | tf_op jit(solution)/shard_map/pallas_call | solution.py:538
  278.5 41.0 %shard_map.180 = (bf16[2,768,3072]{2,1,0:T(8,128)(2,1)}, f32[2,768,3072]{2,1,0:T(8,128)}, f32[2,768,3072]{2,1,0:T(8,128)}) custom-call(bf16[2,768,3072]{2,1,0:T(8,128)(2,1)} %w.4, f32[2,768,3072]{2,1,0:T(8,128)} %m.4, f32[2,768,3072]{2,1,0:T(8,128)} %v.4, bf16[6,18432,128]{2,1,0:T(8,128)(2,1)} %shard_map.178.refs_0_.refs_1_, ...), custom_call_target="tpu_custom_call" | custom-call | tf_op jit(solution)/shard_map/pallas_call | solution.py:538
  319.5 41.0 %shard_map.179 = (bf16[2,768,3072]{2,1,0:T(8,128)(2,1)}, f32[2,768,3072]{2,1,0:T(8,128)}, f32[2,768,3072]{2,1,0:T(8,128)}) custom-call(bf16[2,768,3072]{2,1,0:T(8,128)(2,1)} %w.3, f32[2,768,3072]{2,1,0:T(8,128)} %m.3, f32[2,768,3072]{2,1,0:T(8,128)} %v.3, bf16[6,18432,128]{2,1,0:T(8,128)(2,1)} %shard_map.178.refs_0_.refs_1_, ...), custom_call_target="tpu_custom_call" | custom-call | tf_op jit(solution)/shard_map/pallas_call | solution.py:538

commit v3 on v2

--- a/solution.py
+++ b/solution.py
@@ -45,32 +45,34 @@
         self.m_ag1 = self.m_ag2 + 2 * h2
         self.m_pair = self.m_ag1 + 2 * h1
         self.nmsg = self.m_pair + 1
-    def scratch(self, NB):
-        return [pltpu.VMEM((NB, (self.n1 - 1) * self.L, LANES), BF16),
-                pltpu.VMEM((NB, self.L, LANES), F32),
-                pltpu.VMEM((NB, self.L, LANES), BF16),
-                pltpu.VMEM((NB, (self.n2 - 1) * self.L2, LANES), BF16),
-                pltpu.VMEM((NB, self.L2, LANES), F32),
-                pltpu.VMEM((NB, self.n3, self.L2, LANES), BF16),
-                pltpu.SemaphoreType.DMA((NB, self.nmsg)), pltpu.SemaphoreType.DMA((NB, self.nmsg))]
+    def scratch(self, N):
+        return [pltpu.VMEM((N["R1"], (self.n1 - 1) * self.L, LANES), BF16),
+                pltpu.VMEM((N["O1"], self.L, LANES), F32),
+                pltpu.VMEM((N["O1b"], self.L, LANES), BF16),
+                pltpu.VMEM((N["R2"], (self.n2 - 1) * self.L2, LANES), BF16),
+                pltpu.VMEM((N["O2"], self.L2, LANES), F32),
+                pltpu.VMEM((N["Y"], self.n3, self.L2, LANES), BF16),
+                pltpu.SemaphoreType.DMA((N["S"], self.nmsg)), pltpu.SemaphoreType.DMA((N["S"], self.nmsg))]
 
 def m16(v):
     return pl.multiple_of(v, 16)
 
 class Comm:
-    def __init__(self, n, cfg, B, NB, ND=None):
-        self.n, self.B, self.NB, self.ND = n, B, NB, ND or NB
+    def __init__(self, n, cfg, B, slots):
+        self.n, self.B, self.N = n, B, slots
+        self.ND = slots["D"]
         off, self.colors = 0, []
         for name, rows, dims in cfg:
             self.colors.append(Color(name, off, rows, dims, n)); off += rows
         self.HB, self.TB = off, 2 * off
     def scratch(self):
-        out = [pltpu.VMEM((self.B, self.TB, LANES), BF16), pltpu.VMEM((self.ND, self.HB, LANES), BF16),
+        out = [pltpu.VMEM((self.ND, self.HB, LANES), BF16),
                pltpu.SemaphoreType.DMA((self.ND,)), pltpu.SemaphoreType.DMA((self.ND,))]
         for c in self.colors:
-            out += c.scratch(self.NB)
+            out += c.scratch(self.N)
         return out
-    def setup(self, scratch):
+    def setup(self, G, scratch):
+        self.G = G
         n = self.n
         me = lax.axis_index("dp")
         core = lax.rem(me, 2); z = lax.rem(lax.div(me, 2), n["z"])
@@ -83,9 +85,9 @@
             return me + (q - self.pos[d]) * stride[d]
         self.shifted = shifted
         self.partner = me + 1 - 2 * core
-        self.G, self.D, self.ds, self.dr = scratch[:4]
+        self.D, self.ds, self.dr = scratch[:3]
         self.bufs = {}
-        rest = scratch[4:]
+        rest = scratch[3:]
         for i, c in enumerate(self.colors):
             self.bufs[c.name] = rest[8 * i:8 * i + 8]
         self.mine = core * self.HB
@@ -125,7 +127,7 @@
     def color_phases(self, c):
         G, D = self.G, self.D
         R1, O1, O1b, R2, O2, Y, SS, RS = self.bufs[c.name]
-        NB = self.NB
+        N = self.N
         p1, p2, p3 = (self.pos[d] for d in c.dims)
         r1, l1 = self.shifted(c.dims[0], 1), self.shifted(c.dims[0], -1)
         r2, l2 = self.shifted(c.dims[1], 1), self.shifted(c.dims[1], -1)
@@ -134,21 +136,21 @@
         mod = lambda v, n: lax.rem(v + 4 * n, n)
         base = self.mine + c.off
         dbase = c.off
-        sl = lambda b: lax.rem(b, NB)
-        dsl = lambda b: lax.rem(b, self.ND)
+        at_ = lambda name: (lambda b: lax.rem(b, N[name]))
+        sR1, sO1, sO1b, sR2, sO2, sY, sl, dsl = (at_(k) for k in ("R1", "O1", "O1b", "R2", "O2", "Y", "S", "D"))
 
         def ring(stage):
             if stage == 1:
-                return dict(n=n1, h=h1, L=L, La=La, Lb=Lb, p=p1, right=r1, left=l1, R=R1, m=c.m_rs1)
-            return dict(n=n2, h=h2, L=L2, La=La2, Lb=Lb2, p=p2, right=r2, left=l2, R=R2, m=c.m_rs2)
+                return dict(n=n1, h=h1, L=L, La=La, Lb=Lb, p=p1, right=r1, left=l1, R=R1, sR=sR1, m=c.m_rs1)
+            return dict(n=n2, h=h2, L=L2, La=La2, Lb=Lb2, p=p2, right=r2, left=l2, R=R2, sR=sR2, m=c.m_rs2)
         def local(stage, b, row, k):
             if stage == 1:
                 return G[b, pl.ds(m16(base + row), k), :].astype(F32) + D[dsl(b), pl.ds(m16(dbase + row), k), :].astype(F32)
-            return O1[sl(b), pl.ds(m16(row), k), :] + R1[sl(b), pl.ds(m16(2 * (h1 - 1) * L + row), k), :].astype(F32)
+            return O1[sO1(b), pl.ds(m16(row), k), :] + R1[sR1(b), pl.ds(m16(2 * (h1 - 1) * L + row), k), :].astype(F32)
         def staged(stage, b, row, k):
             if stage == 1:
                 return D.at[dsl(b), pl.ds(m16(dbase + row), k)]
-            return O1b.at[sl(b), pl.ds(m16(row), k)]
+            return O1b.at[sO1b(b), pl.ds(m16(row), k)]
         def rs_copy(stage, b, k, direction):
             g = ring(stage)
             n, h, LL, A, Bb = g["n"], g["h"], g["L"], g["La"], g["Lb"]
@@ -156,13 +158,13 @@
             if k < h:
                 slot = mod(g["p"] + h - k + 1, n) if direction == 0 else mod(g["p"] - h + k, n)
                 src = staged(stage, b, slot * LL, LL)
-                dst = g["R"].at[s, pl.ds((k - 1) * 2 * LL + direction * LL, LL)]
+                dst = g["R"].at[g["sR"](b), pl.ds((k - 1) * 2 * LL + direction * LL, LL)]
             elif direction == 0:
                 src = staged(stage, b, mod(g["p"] + 1, n) * LL + A, Bb)
-                dst = g["R"].at[s, pl.ds((h - 1) * 2 * LL, Bb)]
+                dst = g["R"].at[g["sR"](b), pl.ds((h - 1) * 2 * LL, Bb)]
             else:
                 src = staged(stage, b, g["p"] * LL, A)
-                dst = g["R"].at[s, pl.ds((h - 1) * 2 * LL + Bb, A)]
+                dst = g["R"].at[g["sR"](b), pl.ds((h - 1) * 2 * LL + Bb, A)]
             m = g["m"] + 2 * (k - 1) + direction
             return self.copy(src, dst, SS.at[s, m], RS.at[s, m], g["right"] if direction == 0 else g["left"])
         def rs_step(stage, k):
@@ -178,7 +180,7 @@
                     def total(row, at, kk):
                         v = local(stage, b, row, kk)
                         if k > 1:
-                            v = v + g["R"][s, pl.ds(m16(rin + at), kk), :].astype(F32)
+                            v = v + g["R"][g["sR"](b), pl.ds(m16(rin + at), kk), :].astype(F32)
                         return v
                     def send_part(lo, cnt):
                         def body(i, kk):
@@ -186,12 +188,12 @@
                             if stage == 1:
                                 D[dsl(b), pl.ds(m16(dbase + slot * LL + lo + i), kk), :] = v.astype(BF16)
                             else:
-                                O1b[s, pl.ds(m16(slot * LL + lo + i), kk), :] = v.astype(BF16)
+                                O1b[sO1b(b), pl.ds(m16(slot * LL + lo + i), kk), :] = v.astype(BF16)
                         over_rows(cnt, body)
                     def keep_part(lo, cnt, to):
-                        ref = O1 if stage == 1 else O2
+                        ref, so = (O1, sO1(b)) if stage == 1 else (O2, sO2(b))
                         def body(i, kk):
-                            ref[s, pl.ds(m16(to + i), kk), :] = total(slot * LL + lo + i, lo + i, kk)
+                            ref[so, pl.ds(m16(to + i), kk), :] = total(slot * LL + lo + i, lo + i, kk)
                         over_rows(cnt, body)
                     if k < h:
                         send_part(0, LL)
@@ -213,16 +215,16 @@
         def y_copy(b, k):
             s = sl(b)
             m = c.m_y + k - 1
-            return self.copy(Y.at[s, p3], Y.at[s, p3], SS.at[s, m], RS.at[s, m], self.shifted(c.dims[2], k))
+            return self.copy(Y.at[sY(b), p3], Y.at[sY(b), p3], SS.at[s, m], RS.at[s, m], self.shifted(c.dims[2], k))
         def y_wait(b, k):
             s = sl(b)
             m = c.m_y + k - 1
-            return self.copy(Y.at[s, p3], Y.at[s, mod(p3 - k, n3)], SS.at[s, m], RS.at[s, m], self.shifted(c.dims[2], k))
+            return self.copy(Y.at[sY(b), p3], Y.at[sY(b), mod(p3 - k, n3)], SS.at[s, m], RS.at[s, m], self.shifted(c.dims[2], k))
         def y_send(b):
             s = sl(b)
             def body(i, kk):
-                v = O2[s, pl.ds(i, kk), :] + R2[s, pl.ds(m16(2 * (h2 - 1) * L2 + i), kk), :].astype(F32)
-                Y[s, p3, pl.ds(i, kk), :] = v.astype(BF16)
+                v = O2[sO2(b), pl.ds(i, kk), :] + R2[sR2(b), pl.ds(m16(2 * (h2 - 1) * L2 + i), kk), :].astype(F32)
+                Y[sY(b), p3, pl.ds(i, kk), :] = v.astype(BF16)
             over_rows(L2, body)
             for k in range(1, n3):
                 y_copy(b, k).start()
@@ -234,9 +236,9 @@
                 y_wait(b, k).wait()
             def part(src, cnt, row):
                 def body(i, kk):
-                    v = Y[s, 0, pl.ds(m16(src + i), kk), :].astype(F32)
+                    v = Y[sY(b), 0, pl.ds(m16(src + i), kk), :].astype(F32)
                     for j in range(1, n3):
-                        v = v + Y[s, j, pl.ds(m16(src + i), kk), :].astype(F32)
+                        v = v + Y[sY(b), j, pl.ds(m16(src + i), kk), :].astype(F32)
                     G[b, pl.ds(m16(row + i), kk), :] = v.astype(BF16)
                 over_rows(cnt, body)
             part(0, Lb2, grow(p2 * L2 + La2))
@@ -310,7 +312,7 @@
 TOK, DIM, FF = 1024, 768, 3072
 TF = 256
 NT = FF // TF
-PARTS = 3
+PARTS = 6
 K = NT // PARTS
 HALF = 512
 
@@ -320,15 +322,15 @@
     return lax.dot_general(a, b, (((1,), (1,)), ((), ())), preferred_element_type=F32)
 
 OFFS = {
-    "A": [0, 1, 3, 4, 5, 6, 7, 8, 9, 10, 11, 12, 13, 14, 16, 17],
+    "A": [0, 1, 4, 5, 6, 7, 8, 9, 10, 11, 12, 13, 14, 15, 18, 19],
     "B": [0, 1, 3, 4, 5, 6, 7, 8, 9, 10, 11, 12, 13, 14, 16, 17],
-    "C": [0, 1, 2, 3, 4, 6, 7, 8, 9, 10, 11, 12, 13, 14, 16, 17],
+    "C": [0, 1, 2, 3, 5, 7, 8, 9, 10, 11, 12, 13, 14, 15, 17, 18],
 }
-
-def mega(comm, x_hbm, dy_hbm, wg_hbm, wu_hbm, wd_hbm, o_hbm, A, AT, DY, DYT, H, ACC, TH, TG, TU, WG, WU, WD, wsem, xsem, osem, *cs):
+SLOTS = {"R1": 4, "O1": 2, "O1b": 2, "R2": 3, "O2": 2, "Y": 2, "D": 5, "S": 12}
+
+def mega(comm, x_hbm, dy_hbm, wg_hbm, wu_hbm, wd_hbm, G, A, AT, DY, DYT, H, ACC, TH, TG, TU, WG, WU, WD, wsem, xsem, *cs):
     B = comm.B
-    comm.setup(cs)
-    G = comm.G
+    comm.setup(G, cs)
     def wcopies(u):
         q = lax.div(u, NT)
         layer = lax.rem(q, 2)
@@ -442,7 +444,6 @@
             AT[:, r] = a.T
         each(128, again)
 
-    store = lambda b: pltpu.make_async_copy(G.at[b], o_hbm.at[b], osem.at[b])
     phases = comm.phases()
     events = []
     for ph, fns in enumerate(phases):
@@ -456,7 +457,6 @@
             for name, f in zip(cols, fs):
                 events.append((OFFS[name][ph], f))
     last = max(o for o, _ in events)
-    events.append((last, lambda b: store(b).start()))
     depth = last // K + 1
     def tick(t):
         it = lax.div(t, K) - 1
@@ -487,72 +487,154 @@
             backward(t + NT, t, False)
         return 0
     lax.fori_loop(0, K * B + last + 1, step, 0)
-    def fin(b, _):
-        store(b).wait()
-        return 0
-    lax.fori_loop(0, B, fin, 0)
-
-def gradients(comm, x, dy, wg, wu, wd, vmem=66_900_000):
+
+def gradients(comm, x, dy, wg, wu, wd, vmem=37_000_000):
     V = pltpu.VMEM
     scratch = [V((TOK, DIM), BF16), V((DIM, TOK), BF16), V((TOK, DIM), BF16), V((DIM, TOK), BF16), V((TOK, DIM), BF16), V((TOK, DIM), F32),
                V((TOK, TF), BF16), V((TOK, TF), BF16), V((TOK, TF), BF16),
                V((2, DIM, TF), BF16), V((2, DIM, TF), BF16), V((2, TF, DIM), BF16),
-               pltpu.SemaphoreType.DMA((2, 3)), pltpu.SemaphoreType.DMA((2,)), pltpu.SemaphoreType.DMA((comm.B,))]
+               pltpu.SemaphoreType.DMA((2, 3)), pltpu.SemaphoreType.DMA((2,))]
     return pl.pallas_call(
         functools.partial(mega, comm),
-        out_shape=jax.ShapeDtypeStruct((comm.B, comm.TB, LANES), BF16),
-        in_specs=[pl.BlockSpec(memory_space=pl.ANY)] * 5, out_specs=pl.BlockSpec(memory_space=pl.ANY),
+        out_shape=pltpu.VMEM((comm.B, comm.TB, LANES), BF16),
+        in_specs=[pl.BlockSpec(memory_space=pl.ANY)] * 5, out_specs=pl.BlockSpec(memory_space=pltpu.VMEM),
         scratch_shapes=scratch + comm.scratch(),
         compiler_params=pltpu.CompilerParams(collective_id=0, has_side_effects=True, vmem_limit_bytes=vmem),
     )(x, dy, wg, wu, wd)
 
-def adam_kernel(turned, w, m, v, *refs):
-    gs, (w2, m2, v2) = refs[:-3], refs[-3:]
-    for k, g in enumerate(gs):
-        gv = g[0].astype(F32)
-        if turned:
-            gv = gv.T
-            at = (0, pl.ds(k * LANES, LANES), slice(None))
+def adam_all(weights, m, v, g, parts, layers=2, wide=256, nbuf=4, g_vmem=True, ahead=2, light=False):
+    dim, ff = weights[0].shape[1:]
+    c = wide // LANES
+    per = ff // parts // wide
+    steps = ff // wide
+    cols = ff // parts // LANES
+    S = layers * steps
+    def body(wg, wu, wd, mg, mu, md, vg, vu, vd, gr, owg, owu, owd, omg, omu, omd, ovg, ovu, ovd,
+             wb, mb, vb, xw, xm, xv, dwb, dmb, dvb, dxw, dxm, dxv, *rest):
+        if g_vmem:
+            isem, osem, disem, dosem = rest
         else:
-            at = (0, slice(None), pl.ds(k * LANES, LANES))
-        mm = 0.9 * m[at] + 0.1 * gv
-        vv = 0.95 * v[at] + 0.05 * gv * gv
-        ww = w[at].astype(F32)
-        step = mm * lax.rsqrt(vv + 1e-8) + 0.1 * ww
-        w2[at] = (ww - 0.02 * step).astype(BF16)
-        m2[at] = mm
-        v2[at] = vv
-
-def adam(which, w, m, v, g, c=2):
-    turned = which == 2
-    wide = c * LANES
-    per = FF // PARTS // wide
-    if turned:
-        spec = pl.BlockSpec((1, wide, DIM), lambda l, i: (l, i, 0))
-    else:
-        spec = pl.BlockSpec((1, DIM, wide), lambda l, i: (l, 0, i))
-    def gspec(k):
-        def index(l, i):
-            return ((1 - l) * PARTS + i // per, which * (FF // PARTS // LANES) + (i % per) * c + k, 0)
-        return pl.BlockSpec((1, DIM, LANES), index)
-    return pl.pallas_call(
-        functools.partial(adam_kernel, turned),
-        grid=(2, FF // wide),
-        out_shape=(jax.ShapeDtypeStruct(w.shape, BF16), jax.ShapeDtypeStruct(m.shape, F32), jax.ShapeDtypeStruct(v.shape, F32)),
-        in_specs=[spec] * 3 + [gspec(k) for k in range(c)], out_specs=(spec,) * 3,
-        compiler_params=pltpu.CompilerParams(vmem_limit_bytes=60_000_000),
-    )(w, m, v, *([g] * c))
+            gb, dgb, isem, osem, disem, dosem = rest
+        def where(i):
+            l = lax.div(i, steps)
+            j = lax.rem(i, steps)
+            return l, j, (layers - 1 - l) * parts + lax.div(j, per), lax.rem(j, per) * c
+        def side(l, j):
+            return (l, slice(None), pl.ds(pl.multiple_of(j * wide, wide), wide))
+        def tall(l, j):
+            return (l, pl.ds(pl.multiple_of(j * wide, wide), wide), slice(None))
+        sets = {
+            0: (wg, mg, vg, owg, omg, ovg), 1: (wu, mu, vu, owu, omu, ovu), 2: (wd, md, vd, owd, omd, ovd)}
+        def ins(which, i):
+            l, j, b, cb = where(i)
+            at = tall(l, j) if which == 2 else side(l, j)
+            bufs = (dwb, dmb, dvb) if which == 2 else (wb, mb, vb)
+            sem = disem if which == 2 else isem
+            s = lax.rem(i, nbuf) if which == 2 else lax.rem(i + which * S, nbuf)
+            out = [pltpu.make_async_copy(sets[which][k].at[at], bufs[k].at[s], sem.at[s, k]) for k in range(3)]
+            if not g_vmem:
+                out.append(pltpu.make_async_copy(gr.at[b, pl.ds(pl.multiple_of((which * cols + cb) * dim, dim), c * dim)], (dgb if which == 2 else gb).at[s], sem.at[s, 3]))
+            return out
+        def outs(which, i):
+            l, j, b, cb = where(i)
+            at = tall(l, j) if which == 2 else side(l, j)
+            bufs = (dxw, dxm, dxv) if which == 2 else (xw, xm, xv)
+            sem = dosem if which == 2 else osem
+            s = lax.rem(i, 2) if which == 2 else lax.rem(i + which * S, 2)
+            return [pltpu.make_async_copy(bufs[k].at[s], sets[which][3 + k].at[at], sem.at[s, k]) for k in range(3)]
+        def start(cs):
+            for x in cs:
+                x.start()
+        def wait(cs):
+            for x in cs:
+                x.wait()
+        def compute(which, i):
+            l, j, b, cb = where(i)
+            down = which == 2
+            s = lax.rem(i, nbuf) if down else lax.rem(i + which * S, nbuf)
+            so = lax.rem(i, 2) if down else lax.rem(i + which * S, 2)
+            w_, m_, v_, ow, om, ov = (dwb, dmb, dvb, dxw, dxm, dxv) if down else (wb, mb, vb, xw, xm, xv)
+            for k in range(c):
+                for r in range(0, 256 if light else dim, 256):
+                    if g_vmem:
+                        row = pl.multiple_of((which * cols + cb + k) * dim + r, 128)
+                        gv = gr[b, pl.ds(row, 256), :].astype(F32)
+                    else:
+                        gv = (dgb if down else gb)[s, pl.ds(k * dim + r, 256), :].astype(F32)
+                    if down:
+                        gv = gv.T
+                        at = (pl.ds(k * LANES, LANES), pl.ds(r, 256))
+                    else:
+                        at = (pl.ds(r, 256), pl.ds(k * LANES, LANES))
+                    mm = 0.9 * m_[(s, *at)] + 0.1 * gv
+                    vv = 0.95 * v_[(s, *at)] + 0.05 * gv * gv
+                    ww = w_[(s, *at)].astype(F32)
+                    step = mm * lax.rsqrt(vv + 1e-8) + 0.1 * ww
+                    ow[(so, *at)] = (ww - 0.02 * step).astype(BF16)
+                    om[(so, *at)] = mm
+                    ov[(so, *at)] = vv
+        def whole(i, f):
+            @pl.when(i < S)
+            def _():
+                f(0, i)
+            @pl.when((i >= S) & (i < 2 * S))
+            def _():
+                f(1, i - S)
+        for i in range(ahead):
+            start(ins(0, i))
+        def wide_step(i, _):
+            whole(i + ahead, lambda w, t: start(ins(w, t)))
+            @pl.when(i + ahead >= 2 * S)
+            def _():
+                start(ins(2, i + ahead - 2 * S))
+            whole(i, lambda w, t: wait(ins(w, t)))
+            @pl.when(i >= 2)
+            def _():
+                whole(i - 2, lambda w, t: wait(outs(w, t)))
+            whole(i, lambda w, t: (compute(w, t), start(outs(w, t))))
+            return 0
+        lax.fori_loop(0, 2 * S, wide_step, 0)
+        def tall_step(i, _):
+            @pl.when(i + ahead < S)
+            def _():
+                start(ins(2, i + ahead))
+            wait(ins(2, i))
+            @pl.when(i >= 2)
+            def _():
+                wait(outs(2, i - 2))
+            compute(2, i)
+            start(outs(2, i))
+            return 0
+        lax.fori_loop(0, S, tall_step, 0)
+        for i in (S - 2, S - 1):
+            wait(outs(1, i))
+            wait(outs(2, i))
+    V, D = pltpu.VMEM, pltpu.SemaphoreType.DMA
+    scratch = []
+    for shape in ((dim, wide), (wide, dim)):
+        scratch += [V((nbuf, *shape), BF16), V((nbuf, *shape), F32), V((nbuf, *shape), F32), V((2, *shape), BF16), V((2, *shape), F32), V((2, *shape), F32)]
+    if not g_vmem:
+        scratch += [V((nbuf, c * dim, LANES), BF16)] * 2
+    scratch += [D((nbuf, 4)), D((2, 3)), D((nbuf, 4)), D((2, 3))]
+    anys = pl.BlockSpec(memory_space=pl.ANY)
+    out = pl.pallas_call(
+        body,
+        out_shape=[jax.ShapeDtypeStruct(x.shape, x.dtype) for x in (*weights, *m, *v)],
+        in_specs=[anys] * 9 + [pl.BlockSpec(memory_space=pltpu.VMEM if g_vmem else pl.ANY)],
+        out_specs=[anys] * 9, scratch_shapes=scratch,
+        compiler_params=pltpu.CompilerParams(vmem_limit_bytes=30_000_000 if g_vmem else 60_000_000),
+    )(*weights, *m, *v, pltpu.with_memory_space_constraint(g, pltpu.VMEM) if g_vmem else g)
+    return tuple(out)
 TILE = 16
-COLORS = (("A", 224 * TILE, "xzy"), ("B", 224 * TILE, "yzx"), ("C", 128 * TILE, "zxy"))
+COLORS = (("A", 96 * TILE, "xzy"), ("B", 128 * TILE, "yzx"), ("C", 64 * TILE, "zxy"))
 SIZES = {"x": 4, "y": 4, "z": 8}
 def make_comm():
-    return Comm(SIZES, COLORS, 2 * PARTS, 2, 3)
+    return Comm(SIZES, COLORS, 2 * PARTS, SLOTS)
 
 def train_step(comm, x, dy, *arrays):
     weights, m, v = (arrays[i:i + 3] for i in (0, 3, 6))
     g = gradients(comm, x[0], dy[0], *weights)
-    new = [adam(i, weights[i], m[i], v[i], g) for i in range(3)]
-    return tuple(one[which] for which in range(3) for one in new)
+    return adam_all(weights, m, v, g, PARTS, nbuf=3)
 
 
 def solution(mesh):

time: 361 us -> 327 us (0.906)
  Pallas kernels: 360 us -> 326 us
    pallas_call x4 -> x2, Pallas kernels: 360 us -> 326 us  [the longest x1 230 us: gradients(): pl.pallas_call(functools.partial(mega, comm), out_shape=pltpu.VMEM((comm....]
where the time goes in v3:
time: 327 us
  Pallas kernels  326 us (100%)
    pallas_call x1, Pallas kernels, gradients(): pl.pallas_call(functools.partial(mega, comm), out_shape=pltpu.VMEM((comm....  230 us
    pallas_call x1, Pallas kernels, adam_all(): pl.pallas_call(body, out_shape=[jax.ShapeDtypeStruct(x.shape, x.dtype) fo...  96 us

profile of v3, /device:TPU:1, one launch (start us, length us, event | category | flops | bytes accessed | tf_op | source)
XLA Modules:
  0.0 327.0 jit_solution(13357475483155171399)
XLA Ops:
  0.6 230.2 %shard_map.178.gr = bf16[12,9216,128]{2,1,0:T(8,128)(2,1)S(1)} custom-call(bf16[1024,768]{1,0:T(8,128)(2,1)} %bitcast.2, bf16[1024,768]{1,0:T(8,128)(2,1)} %bitcast.3, bf16[2,768,3072]{2,1,0:T(8,128)(2,1)} %wg.1, bf16[2,768,3072]{2,1,0:T(8,128)(2,1)} %wu.1, bf16[2,3072,768]{2,1,0:T(8,128)(2,1)} %wd.1), custom_call_target="tpu_custom_call" | custom-call | tf_op jit(solution)/shard_map/pallas_call | solution.py:497
  230.9 96.0 %shard_map.179 = (bf16[2,768,3072]{2,1,0:T(8,128)(2,1)}, bf16[2,768,3072]{2,1,0:T(8,128)(2,1)}, bf16[2,3072,768]{2,1,0:T(8,128)(2,1)}, f32[2,768,3072]{2,1,0:T(8...) custom-call(bf16[2,768,3072]{2,1,0:T(8,128)(2,1)} %wg.1, ...), custom_call_target="tpu_custom_call" | custom-call | tf_op jit(solution)/shard_map/pallas_call | solution.py:620

commit v4 on v3

--- a/solution.py
+++ b/solution.py
@@ -502,46 +502,29 @@
         compiler_params=pltpu.CompilerParams(collective_id=0, has_side_effects=True, vmem_limit_bytes=vmem),
     )(x, dy, wg, wu, wd)
 
-def adam_all(weights, m, v, g, parts, layers=2, wide=256, nbuf=4, g_vmem=True, ahead=2, light=False):
+def adam_all(weights, m, v, g, parts, rows=256, nbuf=4, nout=2, ahead=3, layers=2):
     dim, ff = weights[0].shape[1:]
-    c = wide // LANES
-    per = ff // parts // wide
-    steps = ff // wide
-    cols = ff // parts // LANES
-    S = layers * steps
-    def body(wg, wu, wd, mg, mu, md, vg, vu, vd, gr, owg, owu, owd, omg, omu, omd, ovg, ovu, ovd,
-             wb, mb, vb, xw, xm, xv, dwb, dmb, dvb, dxw, dxm, dxv, *rest):
-        if g_vmem:
-            isem, osem, disem, dosem = rest
-        else:
-            gb, dgb, isem, osem, disem, dosem = rest
-        def where(i):
-            l = lax.div(i, steps)
-            j = lax.rem(i, steps)
-            return l, j, (layers - 1 - l) * parts + lax.div(j, per), lax.rem(j, per) * c
-        def side(l, j):
-            return (l, slice(None), pl.ds(pl.multiple_of(j * wide, wide), wide))
-        def tall(l, j):
-            return (l, pl.ds(pl.multiple_of(j * wide, wide), wide), slice(None))
-        sets = {
-            0: (wg, mg, vg, owg, omg, ovg), 1: (wu, mu, vu, owu, omu, ovu), 2: (wd, md, vd, owd, omd, ovd)}
-        def ins(which, i):
-            l, j, b, cb = where(i)
-            at = tall(l, j) if which == 2 else side(l, j)
-            bufs = (dwb, dmb, dvb) if which == 2 else (wb, mb, vb)
-            sem = disem if which == 2 else isem
-            s = lax.rem(i, nbuf) if which == 2 else lax.rem(i + which * S, nbuf)
-            out = [pltpu.make_async_copy(sets[which][k].at[at], bufs[k].at[s], sem.at[s, k]) for k in range(3)]
-            if not g_vmem:
-                out.append(pltpu.make_async_copy(gr.at[b, pl.ds(pl.multiple_of((which * cols + cb) * dim, dim), c * dim)], (dgb if which == 2 else gb).at[s], sem.at[s, 3]))
-            return out
-        def outs(which, i):
-            l, j, b, cb = where(i)
-            at = tall(l, j) if which == 2 else side(l, j)
-            bufs = (dxw, dxm, dxv) if which == 2 else (xw, xm, xv)
-            sem = dosem if which == 2 else osem
-            s = lax.rem(i, 2) if which == 2 else lax.rem(i + which * S, 2)
-            return [pltpu.make_async_copy(bufs[k].at[s], sets[which][3 + k].at[at], sem.at[s, k]) for k in range(3)]
+    blocks = dim // LANES
+    per = ff // parts // LANES
+    down_tiles = ff // rows
+    across = ff // dim
+    S = layers * down_tiles
+    def body(wg, wu, wd, mg, mu, md, vg, vu, vd, gr, owg, owu, owd, omg, omu, omd, ovg, ovu, ovd, wb, mb, vb, xw, xm, xv, isem, osem):
+        ins_, outs_ = ((wg, mg, vg), (wu, mu, vu), (wd, md, vd)), ((owg, omg, ovg), (owu, omu, ovu), (owd, omd, ovd))
+        def place(which, i):
+            l, j = lax.div(i, down_tiles), lax.rem(i, down_tiles)
+            if which == 2:
+                return l, j * rows, 0
+            return l, lax.div(j, across) * rows, lax.rem(j, across) * dim
+        def at(which, i):
+            l, r, c = place(which, i)
+            return (l, pl.ds(pl.multiple_of(r, rows), rows), pl.ds(pl.multiple_of(c, dim), dim))
+        def load(which, i):
+            s = lax.rem(i + which * S, nbuf)
+            return [pltpu.make_async_copy(ins_[which][k].at[at(which, i)], b.at[s], isem.at[s, k]) for k, b in enumerate((wb, mb, vb))]
+        def store(which, i):
+            s = lax.rem(i + which * S, nout)
+            return [pltpu.make_async_copy(b.at[s], outs_[which][k].at[at(which, i)], osem.at[s, k]) for k, b in enumerate((xw, xm, xv))]
         def start(cs):
             for x in cs:
                 x.start()
@@ -549,81 +532,57 @@
             for x in cs:
                 x.wait()
         def compute(which, i):
-            l, j, b, cb = where(i)
-            down = which == 2
-            s = lax.rem(i, nbuf) if down else lax.rem(i + which * S, nbuf)
-            so = lax.rem(i, 2) if down else lax.rem(i + which * S, 2)
-            w_, m_, v_, ow, om, ov = (dwb, dmb, dvb, dxw, dxm, dxv) if down else (wb, mb, vb, xw, xm, xv)
-            for k in range(c):
-                for r in range(0, 256 if light else dim, 256):
-                    if g_vmem:
-                        row = pl.multiple_of((which * cols + cb + k) * dim + r, 128)
-                        gv = gr[b, pl.ds(row, 256), :].astype(F32)
-                    else:
-                        gv = (dgb if down else gb)[s, pl.ds(k * dim + r, 256), :].astype(F32)
-                    if down:
-                        gv = gv.T
-                        at = (pl.ds(k * LANES, LANES), pl.ds(r, 256))
-                    else:
-                        at = (pl.ds(r, 256), pl.ds(k * LANES, LANES))
-                    mm = 0.9 * m_[(s, *at)] + 0.1 * gv
-                    vv = 0.95 * v_[(s, *at)] + 0.05 * gv * gv
-                    ww = w_[(s, *at)].astype(F32)
-                    step = mm * lax.rsqrt(vv + 1e-8) + 0.1 * ww
-                    ow[(so, *at)] = (ww - 0.02 * step).astype(BF16)
-                    om[(so, *at)] = mm
-                    ov[(so, *at)] = vv
-        def whole(i, f):
-            @pl.when(i < S)
-            def _():
-                f(0, i)
-            @pl.when((i >= S) & (i < 2 * S))
-            def _():
-                f(1, i - S)
+            l, r, c = place(which, i)
+            s, so = lax.rem(i + which * S, nbuf), lax.rem(i + which * S, nout)
+            def one(gv, where):
+                mm = 0.9 * mb[(s, *where)] + 0.1 * gv
+                vv = 0.95 * vb[(s, *where)] + 0.05 * gv * gv
+                ww = wb[(s, *where)].astype(F32)
+                step = mm * lax.rsqrt(vv + 1e-8) + 0.1 * ww
+                xw[(so, *where)] = (ww - 0.02 * step).astype(BF16)
+                xm[(so, *where)] = mm
+                xv[(so, *where)] = vv
+            first = (layers - 1 - l) * parts
+            if which < 2:
+                for k in range(blocks):
+                    col = lax.div(c, LANES) + k
+                    b = first + lax.div(col, per)
+                    row = (which * per + lax.rem(col, per)) * dim + r
+                    one(gr[b, pl.ds(pl.multiple_of(row, rows), rows), :].astype(F32), (slice(None), pl.ds(k * LANES, LANES)))
+            else:
+                for k in range(rows // LANES):
+                    col = lax.div(r, LANES) + k
+                    b = first + lax.div(col, per)
+                    for q in range(0, dim, 256):
+                        row = (which * per + lax.rem(col, per)) * dim + q
+                        one(gr[b, pl.ds(pl.multiple_of(row, 256), 256), :].astype(F32).T, (pl.ds(k * LANES, LANES), pl.ds(q, 256)))
+        def each(i, f):
+            for which in range(3):
+                @pl.when((i >= which * S) & (i < (which + 1) * S))
+                def _():
+                    f(which, i - which * S)
         for i in range(ahead):
-            start(ins(0, i))
-        def wide_step(i, _):
-            whole(i + ahead, lambda w, t: start(ins(w, t)))
-            @pl.when(i + ahead >= 2 * S)
-            def _():
-                start(ins(2, i + ahead - 2 * S))
-            whole(i, lambda w, t: wait(ins(w, t)))
-            @pl.when(i >= 2)
-            def _():
-                whole(i - 2, lambda w, t: wait(outs(w, t)))
-            whole(i, lambda w, t: (compute(w, t), start(outs(w, t))))
+            start(load(0, i))
+        def step(i, _):
+            each(i + ahead, lambda w, t: start(load(w, t)))
+            each(i, lambda w, t: wait(load(w, t)))
+            each(i - nout, lambda w, t: wait(store(w, t)))
+            each(i, lambda w, t: (compute(w, t), start(store(w, t))))
             return 0
-        lax.fori_loop(0, 2 * S, wide_step, 0)
-        def tall_step(i, _):
-            @pl.when(i + ahead < S)
-            def _():
-                start(ins(2, i + ahead))
-            wait(ins(2, i))
-            @pl.when(i >= 2)
-            def _():
-                wait(outs(2, i - 2))
-            compute(2, i)
-            start(outs(2, i))
-            return 0
-        lax.fori_loop(0, S, tall_step, 0)
-        for i in (S - 2, S - 1):
-            wait(outs(1, i))
-            wait(outs(2, i))
+        lax.fori_loop(0, 3 * S, step, 0)
+        for i in range(S - nout, S):
+            wait(store(2, i))
     V, D = pltpu.VMEM, pltpu.SemaphoreType.DMA
-    scratch = []
-    for shape in ((dim, wide), (wide, dim)):
-        scratch += [V((nbuf, *shape), BF16), V((nbuf, *shape), F32), V((nbuf, *shape), F32), V((2, *shape), BF16), V((2, *shape), F32), V((2, *shape), F32)]
-    if not g_vmem:
-        scratch += [V((nbuf, c * dim, LANES), BF16)] * 2
-    scratch += [D((nbuf, 4)), D((2, 3)), D((nbuf, 4)), D((2, 3))]
+    t = (rows, dim)
     anys = pl.BlockSpec(memory_space=pl.ANY)
     out = pl.pallas_call(
         body,
         out_shape=[jax.ShapeDtypeStruct(x.shape, x.dtype) for x in (*weights, *m, *v)],
-        in_specs=[anys] * 9 + [pl.BlockSpec(memory_space=pltpu.VMEM if g_vmem else pl.ANY)],
-        out_specs=[anys] * 9, scratch_shapes=scratch,
-        compiler_params=pltpu.CompilerParams(vmem_limit_bytes=30_000_000 if g_vmem else 60_000_000),
-    )(*weights, *m, *v, pltpu.with_memory_space_constraint(g, pltpu.VMEM) if g_vmem else g)
+        in_specs=[anys] * 9 + [pl.BlockSpec(memory_space=pltpu.VMEM)],
+        out_specs=[anys] * 9,
+        scratch_shapes=[V((nbuf, *t), BF16), V((nbuf, *t), F32), V((nbuf, *t), F32), V((nout, *t), BF16), V((nout, *t), F32), V((nout, *t), F32), D((nbuf, 3)), D((nout, 3))],
+        compiler_params=pltpu.CompilerParams(vmem_limit_bytes=32_000_000),
+    )(*weights, *m, *v, pltpu.with_memory_space_constraint(g, pltpu.VMEM))
     return tuple(out)
 TILE = 16
 COLORS = (("A", 96 * TILE, "xzy"), ("B", 128 * TILE, "yzx"), ("C", 64 * TILE, "zxy"))
@@ -634,7 +593,7 @@
 def train_step(comm, x, dy, *arrays):
     weights, m, v = (arrays[i:i + 3] for i in (0, 3, 6))
     g = gradients(comm, x[0], dy[0], *weights)
-    return adam_all(weights, m, v, g, PARTS, nbuf=3)
+    return adam_all(weights, m, v, g, PARTS, rows=128, nbuf=8, nout=4, ahead=7)
 
 
 def solution(mesh):

time: 327 us -> 321 us (0.982)
  Pallas kernels: 326 us -> 320 us
    pallas_call x1, Pallas kernels: 96 us -> 89.4 us  [adam_all(): pl.pallas_call(body, out_shape=[jax.ShapeDtypeStruct(x.shape, x.dtype) fo...]
where the time goes in v4:
time: 321 us; the launch traced here: 320 us
  Pallas kernels  320 us (100%)
    pallas_call x1, Pallas kernels, gradients(): pl.pallas_call(functools.partial(mega, comm), out_shape=pltpu.VMEM((comm....  230 us
    pallas_call x1, Pallas kernels, adam_all(): pl.pallas_call(body, out_shape=[jax.ShapeDtypeStruct(x.shape, x.dtype) fo...  89.4 us

profile of v4, /device:TPU:1, one launch (start us, length us, event | category | flops | bytes accessed | tf_op | source)
XLA Modules:
  0.0 320.5 jit_solution(2748015992400933104)
XLA Ops:
  0.6 230.2 %shard_map.178.gr = bf16[12,9216,128]{2,1,0:T(8,128)(2,1)S(1)} custom-call(bf16[1024,768]{1,0:T(8,128)(2,1)} %bitcast.2, bf16[1024,768]{1,0:T(8,128)(2,1)} %bitcast.3, bf16[2,768,3072]{2,1,0:T(8,128)(2,1)} %wg.1, bf16[2,768,3072]{2,1,0:T(8,128)(2,1)} %wu.1, bf16[2,3072,768]{2,1,0:T(8,128)(2,1)} %wd.1), custom_call_target="tpu_custom_call" | custom-call | tf_op jit(solution)/shard_map/pallas_call | solution.py:497
  230.9 89.4 %shard_map.179 = (bf16[2,768,3072]{2,1,0:T(8,128)(2,1)}, bf16[2,768,3072]{2,1,0:T(8,128)(2,1)}, bf16[2,3072,768]{2,1,0:T(8,128)(2,1)}, f32[2,768,3072]{2,1,0:T(8...) custom-call(bf16[2,768,3072]{2,1,0:T(8,128)(2,1)} %wg.1, ...), custom_call_target="tpu_custom_call" | custom-call | tf_op jit(solution)/shard_map/pallas_call | solution.py:578
